TPU v7x, 128 devices: a whole 4x4x4 slice. The times are simulated.
128 devices in a mesh: gx: 8 (over z, core), gy: 16 (over x, y).
Axes of the slice: x: 4, y: 4, z: 4, core: 2. Of those that a mesh axis runs over, the one named last changes fastest.
Arguments:
- atm_members: float32 [8, 16, 80, 12, 128], P('gx', 'gy'), may hold values from -6 to 6
- ocean_members: bfloat16 [8, 16, 80, 1024], P('gx', 'gy'), may hold values from -6 to 6
- remap_weights: bfloat16 [8, 16, 4, 1024, 128], P('gx', 'gy'), may hold values from -0.09375 to 0.09375
- pair_src: int32 [8, 16, 4], P('gx', 'gy'), may hold values from 0 to 127, as said below
- obs_cell: int32 [8, 16, 64], P('gx', 'gy'), may hold values from 0 to 127
- obs_value: float32 [8, 16, 64], P('gx', 'gy'), may hold values from -8 to 8
- obs_error: float32 [8, 16, 64], P('gx', 'gy'), may hold values from 2 to 16
- obs_live: int32 [8, 16, 64], P('gx', 'gy'), may hold values from 0 to 1, as said below
- obs_order: int32 [8, 16, 64], P('gx', 'gy'), may hold values from 0 to 63, each once within a row
Outputs:
- post_mean: float32 [8, 16, 13, 128], P('gx', 'gy')
- post_anom: float32 [8, 16, 80, 13, 128], P('gx', 'gy')
Inputs may be any that keep to these rules, and one draw needn't show every extreme that they name: `pair_src`: for atmosphere tile (i, j) the 4 numbers are distinct, each a * 16 + b with |a - i| <= 1 and |b - j| <= 1. `obs_live`: the live slots of a tile are its first ones, between 8 and 64 of them; some tile has all slots live. `obs_order`: each tile's last dimension is a permutation of its slots.
All inputs are finite; a program needn't handle non-finite values.
Results may differ from a plain program's by a relative error of at most 0.0003.
Values may be sent and summed in bfloat16 or wider, within the bound.
A program may use at most 64 MiB of HBM per device.

v0:
```python
import jax
import jax.numpy as jnp
from jax import lax
from jax.sharding import PartitionSpec as P

MEM = 80
AX = 8
AY = 16
OCN_DEV = 1024
OB = 32
NB = 2
K = 4
FIELDS = 12
CELLS = 128
RAD = 2


exact_mode = lax.Precision.HIGHEST


def extended(block, sides, width):
    for axis, dim in sides:
        count = lax.axis_size(axis)
        forward = [(i, i + 1) for i in range(count - 1)]
        backward = [(target, source) for source, target in forward]
        low = lax.ppermute(
            lax.slice_in_dim(block, block.shape[dim] - width, None, axis=dim), axis, forward
        )
        high = lax.ppermute(lax.slice_in_dim(block, 0, width, axis=dim), axis, backward)
        block = jnp.concatenate([low, block, high], axis=dim)
    return block


def update_group(packets, anomaly, base_x, base_y):
    members = anomaly.shape[0]
    components = anomaly.shape[1]
    cell_count = anomaly.shape[2]
    observed = jnp.transpose(packets[:, :members, :], (1, 0, 2)).reshape(members, -1)
    innovation = packets[:, members, :].reshape(-1)
    errors = packets[:, members + 1, :].reshape(-1)
    obs_x = packets[:, members + 2, :].reshape(-1)
    obs_y = packets[:, members + 3, :].reshape(-1)
    live = packets[:, members + 4, :].reshape(-1)
    variance = jnp.sum(observed * observed, axis=0) / (members - 1)
    denominator = variance + errors + (1.0 - live)
    weighting = live / denominator
    damping = 1.0 / (1.0 + jnp.sqrt(errors / denominator))
    cell_index = jnp.arange(cell_count, dtype=jnp.int32)
    cell_x = (base_x + cell_index // AY).astype(jnp.float32)
    cell_y = (base_y + cell_index % AY).astype(jnp.float32)
    distance = (obs_x[:, None] - cell_x[None, :]) ** 2 + (obs_y[:, None] - cell_y[None, :]) ** 2
    taper = jnp.maximum(1.0 - distance / float(RAD * RAD), 0.0) ** 2
    flat_anomaly = anomaly.reshape(members, components * cell_count)
    covariance = jnp.dot(
        observed.T, flat_anomaly, precision=exact_mode, preferred_element_type=jnp.float32
    ) / (members - 1)
    gain = covariance.reshape(-1, components, cell_count) * (taper * weighting[:, None])[:, None, :]
    gain = gain.reshape(-1, components * cell_count)
    mean_step = jnp.dot(
        innovation[None, :], gain, precision=exact_mode, preferred_element_type=jnp.float32
    )
    anomaly_step = jnp.dot(
        observed * damping[None, :], gain, precision=exact_mode, preferred_element_type=jnp.float32
    )
    return (
        mean_step.reshape(components, cell_count),
        anomaly_step.reshape(members, components, cell_count),
    )


def local(
    atm_members,
    ocean_members,
    remap_weights,
    pair_src,
    obs_cell,
    obs_value,
    obs_error,
    obs_live,
    obs_order,
):
    sources = pair_src[0, 0]
    weights = remap_weights[0, 0].reshape(K * OCN_DEV, CELLS)
    row_count = lax.axis_size("gy")
    position = (sources // row_count - lax.axis_index("gx") + 1) * 3 + (
        sources % row_count - lax.axis_index("gy") + 1
    )
    column = extended(ocean_members, (("gx", 0),), 1)
    nearby_rows = extended(column, (("gy", 1),), 1)
    flattened = nearby_rows.reshape(9, MEM * OCN_DEV)
    selector = (position[:, None] == jnp.arange(9, dtype=jnp.int32)[None, :]).astype(jnp.bfloat16)
    chosen = jnp.dot(selector, flattened, preferred_element_type=jnp.float32)
    chosen = chosen.astype(jnp.bfloat16)
    stacked = jnp.transpose(chosen.reshape(K, MEM, OCN_DEV), (1, 0, 2)).reshape(MEM, K * OCN_DEV)
    surface = jnp.dot(stacked, weights, preferred_element_type=jnp.float32)
    state = jnp.concatenate([atm_members[0, 0], surface[:, None, :]], axis=1)
    ens_mean = jnp.sum(state, axis=0) / MEM
    anomaly = state - ens_mean[None]
    base_x = lax.axis_index("gx") * AX
    base_y = lax.axis_index("gy") * AY
    for batch_index in range(NB):
        obs_slots = obs_order[0, 0, batch_index * OB : (batch_index + 1) * OB]
        obs_cells = obs_cell[0, 0][obs_slots]
        observed = anomaly[:, FIELDS, :][:, obs_cells]
        predicted = ens_mean[FIELDS][obs_cells]
        innovation = obs_value[0, 0][obs_slots] - predicted
        errors = obs_error[0, 0][obs_slots]
        pos_x = (base_x + obs_cells // AY).astype(jnp.float32)
        pos_y = (base_y + obs_cells % AY).astype(jnp.float32)
        live = obs_live[0, 0][obs_slots].astype(jnp.float32)
        extras = jnp.stack([innovation, errors, pos_x, pos_y, live], axis=0)
        packet = jnp.concatenate([observed, extras], axis=0)[None, None]
        nearby = extended(packet, (("gx", 0), ("gy", 1)), 1)
        mean_total = jnp.zeros_like(ens_mean)
        anomaly_total = jnp.zeros_like(anomaly)
        for row_index in range(3):
            mean_step, anomaly_step = update_group(nearby[row_index], anomaly, base_x, base_y)
            mean_total = mean_total + mean_step
            anomaly_total = anomaly_total + anomaly_step
        ens_mean = ens_mean + mean_total
        anomaly = anomaly - anomaly_total
    return (ens_mean[None, None], anomaly[None, None])


def solution(mesh):
    in_specs = (
        P("gx", "gy", None, None, None),
        P("gx", "gy", None, None),
        P("gx", "gy", None, None, None),
        P("gx", "gy", None),
        P("gx", "gy", None),
        P("gx", "gy", None),
        P("gx", "gy", None),
        P("gx", "gy", None),
        P("gx", "gy", None),
    )
    out_specs = (P("gx", "gy", None, None), P("gx", "gy", None, None, None))
    return jax.shard_map(local, mesh=mesh, in_specs=in_specs, out_specs=out_specs, check_vma=False)
```

profile of v0, /device:TPU:7, one launch (start us, length us, event | category | flops | bytes accessed | tf_op | source)
XLA Modules:
  0.0 102.3 jit_solution(3507445476075853033)
XLA Ops:
  0.7 4.2 %collective-permute-start = (bf16[1,1,80,1024]{3,2,1,0:T(8,128)(2,1)}, bf16[1,1,80,1024]{3,2,1,0:T(8,128)(2,1)S(1)}, u32[]{:S(2)}, u32[]{:S(2)}) collective-permute-start(bf16[1,1,80,1024]{3,2,1,0:T(8,128)(2,1)} %param.10), channel_id=1, source_target_pairs={{0,16},{16,32},{32,48},{48,64},{64,80},{80,96},{96,112},{1,17},{17... | collective-permute-start | bytes 491528 | tf_op jit(solution)/shard_map/ppermute | solution.py:26
  4.9 1.9 %collective-permute-start.1 = (bf16[1,1,80,1024]{3,2,1,0:T(8,128)(2,1)}, bf16[1,1,80,1024]{3,2,1,0:T(8,128)(2,1)S(1)}, u32[]{:S(2)}, u32[]{:S(2)}) collective-permute-start(bf16[1,1,80,1024]{3,2,1,0:T(8,128)(2,1)} %param.10), channel_id=1, source_target_pairs={{16,0},{32,16},{48,32},{64,48},{80,64},{96,80},{112,96},{17,1},{33... | collective-permute-start | bytes 491528 | tf_op jit(solution)/shard_map/ppermute | solution.py:29
  7.7 1.4 %gather_fusion = s32[32]{0:T(128)S(1)} fusion(s32[64]{0:T(128)} %bitcast.290, s32[1024]{0:T(1024)S(1)} %get-tuple-element.69), kind=kCustom, calls=%fused_computation | custom fusion | bytes 384 | tf_op jit(solution)/shard_map/gather | solution.py:103
  9.0 1.4 %gather_fusion.5 = s32[32]{0:T(128)S(1)} fusion(s32[64]{0:T(128)} %bitcast.292, s32[1024]{0:T(1024)S(1)} %get-tuple-element.69), kind=kCustom, calls=%fused_computation.5 | custom fusion | bytes 384 | tf_op jit(solution)/shard_map/gather | solution.py:110
  10.4 1.4 %gather_fusion.6 = s32[32]{0:T(128)S(1)} fusion(s32[64]{0:T(128)} %bitcast.291, s32[1024]{0:T(1024)S(1)} %get-tuple-element.68), kind=kCustom, calls=%fused_computation.6 | custom fusion | bytes 384 | tf_op jit(solution)/shard_map/gather | solution.py:103
  12.6 3.2 %collective-permute-start.2 = (bf16[3,1,80,1024]{3,2,1,0:T(8,128)(2,1)S(1)}, bf16[3,1,80,1024]{3,2,1,0:T(8,128)(2,1)S(1)}, u32[]{:S(2)}, u32[]{:S(2)}) collective-permute-start(bf16[3,1,80,1024]{3,2,1,0:T(8,128)(2,1)S(1)} %constant_dynamic-update-slice_fusion), channel_id=1, source_target_pairs={{0,1},{1,2},{2,3},{3,4},{4,5},{5,6},{6,7},{7,8},{8,9},{9,10},{10,1... | collective-permute-start | bytes 1474568 | tf_op jit(solution)/shard_map/ppermute | solution.py:26
  15.9 4.2 %collective-permute-start.3 = (bf16[3,1,80,1024]{3,2,1,0:T(8,128)(2,1)S(1)}, bf16[3,1,80,1024]{3,2,1,0:T(8,128)(2,1)S(1)}, u32[]{:S(2)}, u32[]{:S(2)}) collective-permute-start(bf16[3,1,80,1024]{3,2,1,0:T(8,128)(2,1)S(1)} %constant_dynamic-update-slice_fusion), channel_id=1, source_target_pairs={{1,0},{2,1},{3,2},{4,3},{5,4},{6,5},{7,6},{8,7},{9,8},{10,9},{11,1... | collective-permute-start | bytes 1474568 | tf_op jit(solution)/shard_map/ppermute | solution.py:29
  22.5 5.2 %collective-permute-done.2 = bf16[3,1,80,1024]{3,2,1,0:T(8,128)(2,1)S(1)} collective-permute-done((bf16[3,1,80,1024]{3,2,1,0:T(8,128)(2,1)S(1)}, bf16[3,1,80,1024]{3,2,1,0:T(8,128)(2,1)S(1)}, u32[]{:S(2)}, u32[]{:S(2)}) %collective-permute-start.2) | collective-permute-done | bytes 491552 | tf_op jit(solution)/shard_map/ppermute | solution.py:26
  27.7 1.8 %collective-permute-done.3 = bf16[3,1,80,1024]{3,2,1,0:T(8,128)(2,1)S(1)} collective-permute-done((bf16[3,1,80,1024]{3,2,1,0:T(8,128)(2,1)S(1)}, bf16[3,1,80,1024]{3,2,1,0:T(8,128)(2,1)S(1)}, u32[]{:S(2)}, u32[]{:S(2)}) %collective-permute-start.3) | collective-permute-done | bytes 491552 | tf_op jit(solution)/shard_map/ppermute | solution.py:29
  30.0 1.4 %copy.96 = bf16[2,8,80,1024]{3,1,2,0:T(8,128)(2,1)S(1)} copy(bf16[2,8,80,1024]{3,2,1,0:T(8,128)(2,1)S(1)} %bitcast.304) | data formatting | bytes 5242880
  36.1 5.4 %collective-permute-start.4 = (f32[1,1,85,32]{2,3,1,0:T(8,128)S(1)}, f32[1,1,85,32]{2,3,1,0:T(8,128)S(1)}, u32[]{:S(2)}, u32[]{:S(2)}) collective-permute-start(f32[1,1,85,32]{2,3,1,0:T(8,128)S(1)} %bitcast.328), channel_id=1, source_target_pairs={{0,16},{16,32},{32,48},{48,64},{64,80},{80,96},{96,112},{1,17},{17... | collective-permute-start | bytes 32648 | tf_op jit(solution)/shard_map/ppermute | solution.py:26
  41.5 1.9 %collective-permute-start.5 = (f32[1,1,85,32]{2,3,1,0:T(8,128)S(1)}, f32[1,1,85,32]{2,3,1,0:T(8,128)S(1)}, u32[]{:S(2)}, u32[]{:S(2)}) collective-permute-start(f32[1,1,85,32]{2,3,1,0:T(8,128)S(1)} %bitcast.329), channel_id=1, source_target_pairs={{16,0},{32,16},{48,32},{64,48},{80,64},{96,80},{112,96},{17,1},{33... | collective-permute-start | bytes 32648 | tf_op jit(solution)/shard_map/ppermute | solution.py:29
  44.0 2.5 %collective-permute-done.5 = f32[1,1,85,32]{2,3,1,0:T(8,128)S(1)} collective-permute-done((f32[1,1,85,32]{2,3,1,0:T(8,128)S(1)}, f32[1,1,85,32]{2,3,1,0:T(8,128)S(1)}, u32[]{:S(2)}, u32[]{:S(2)}) %collective-permute-start.5) | collective-permute-done | bytes 10912 | tf_op jit(solution)/shard_map/ppermute | solution.py:29
  46.6 3.1 %collective-permute-start.6 = (f32[3,1,85,32]{2,3,1,0:T(8,128)S(1)}, f32[3,1,85,32]{2,3,1,0:T(8,128)S(1)}, u32[]{:S(2)}, u32[]{:S(2)}) collective-permute-start(f32[3,1,85,32]{2,3,1,0:T(8,128)S(1)} %pad_maximum_fusion.4), channel_id=1, source_target_pairs={{0,1},{1,2},{2,3},{3,4},{4,5},{5,6},{6,7},{7,8},{8,9},{9,10},{10,1... | collective-permute-start | bytes 97928 | tf_op jit(solution)/shard_map/ppermute | solution.py:26
  49.7 5.2 %collective-permute-start.7 = (f32[3,1,85,32]{2,3,1,0:T(8,128)S(1)}, f32[3,1,85,32]{2,3,1,0:T(8,128)S(1)}, u32[]{:S(2)}, u32[]{:S(2)}) collective-permute-start(f32[3,1,85,32]{2,3,1,0:T(8,128)S(1)} %pad_maximum_fusion.4), channel_id=1, source_target_pairs={{1,0},{2,1},{3,2},{4,3},{5,4},{6,5},{7,6},{8,7},{9,8},{10,9},{11,1... | collective-permute-start | bytes 97928 | tf_op jit(solution)/shard_map/ppermute | solution.py:29
  54.9 1.3 %gather_fusion.8 = f32[32]{0:T(128)} fusion(f32[64]{0:T(128)S(1)} %bitcast.295, s32[1024]{0:T(1024)S(1)} %get-tuple-element.68), kind=kCustom, calls=%fused_computation.8 | custom fusion | bytes 384 | tf_op jit(solution)/shard_map/gather | solution.py:106
  58.7 0.9 subtract_reduce_fusion.4
  59.7 0.9 subtract_reduce_fusion.5
  63.7 0.8 fusion.6
  65.3 0.8 fusion.7
  66.2 1.7 %fusion.8 = f32[12,13,8,128]{3,2,1,0:T(8,128)S(1)} fusion(f32[80,96]{0,1:T(8,128)S(1)} %bitcast.309, f32[12,8,13,128]{3,2,1,0:T(8,128)S(1)} %bitcast.314, f32[13,128]{1,0:T(8,128)} %copy-done.9, f32[80,1,128]{2,0,1:T(8,128)} %copy-done.8, f32[80,12,128]{2,0,1:T(8,128)S(1)} %bitcast.303), kind=kOutput, calls=%fused_computation.28 | convolution fusion | flops 153939968 | bytes 1847808 | tf_op jit(solution)/shard_map/dot_general | solution.py:54
  70.8 1.0 fusion.31
  74.3 0.8 gather_fusion.9
  76.0 2.2 %collective-permute-start.8 = (f32[1,1,85,32]{2,3,1,0:T(8,128)S(1)}, f32[1,1,85,32]{2,3,1,0:T(8,128)S(1)}, u32[]{:S(2)}, u32[]{:S(2)}) collective-permute-start(f32[1,1,85,32]{2,3,1,0:T(8,128)S(1)} %bitcast.332), channel_id=1, source_target_pairs={{0,16},{16,32},{32,48},{48,64},{64,80},{80,96},{96,112},{1,17},{17... | collective-permute-start | bytes 32648 | tf_op jit(solution)/shard_map/ppermute | solution.py:26
  78.2 2.1 %collective-permute-start.9 = (f32[1,1,85,32]{2,3,1,0:T(8,128)S(1)}, f32[1,1,85,32]{2,3,1,0:T(8,128)S(1)}, u32[]{:S(2)}, u32[]{:S(2)}) collective-permute-start(f32[1,1,85,32]{2,3,1,0:T(8,128)S(1)} %bitcast.333), channel_id=1, source_target_pairs={{16,0},{32,16},{48,32},{64,48},{80,64},{96,80},{112,96},{17,1},{33... | collective-permute-start | bytes 32648 | tf_op jit(solution)/shard_map/ppermute | solution.py:29
  80.3 2.9 %collective-permute-done.9 = f32[1,1,85,32]{2,3,1,0:T(8,128)S(1)} collective-permute-done((f32[1,1,85,32]{2,3,1,0:T(8,128)S(1)}, f32[1,1,85,32]{2,3,1,0:T(8,128)S(1)}, u32[]{:S(2)}, u32[]{:S(2)}) %collective-permute-start.9) | collective-permute-done | bytes 10912 | tf_op jit(solution)/shard_map/ppermute | solution.py:29
  83.2 1.9 %collective-permute-start.10 = (f32[3,1,85,32]{2,3,1,0:T(8,128)S(1)}, f32[3,1,85,32]{2,3,1,0:T(8,128)S(1)}, u32[]{:S(2)}, u32[]{:S(2)}) collective-permute-start(f32[3,1,85,32]{2,3,1,0:T(8,128)S(1)} %pad_maximum_fusion.5), channel_id=1, source_target_pairs={{0,1},{1,2},{2,3},{3,4},{4,5},{5,6},{6,7},{7,8},{8,9},{9,10},{10,1... | collective-permute-start | bytes 97928 | tf_op jit(solution)/shard_map/ppermute | solution.py:26
  85.2 5.7 %collective-permute-start.11 = (f32[3,1,85,32]{2,3,1,0:T(8,128)S(1)}, f32[3,1,85,32]{2,3,1,0:T(8,128)S(1)}, u32[]{:S(2)}, u32[]{:S(2)}) collective-permute-start(f32[3,1,85,32]{2,3,1,0:T(8,128)S(1)} %pad_maximum_fusion.5), channel_id=1, source_target_pairs={{1,0},{2,1},{3,2},{4,3},{5,4},{6,5},{7,6},{8,7},{9,8},{10,9},{11,1... | collective-permute-start | bytes 97928 | tf_op jit(solution)/shard_map/ppermute | solution.py:29
  90.9 0.9 collective-permute-done.11
  95.0 0.8 fusion.9
  97.1 0.8 fusion.10
  100.9 1.4 %fusion.13 = f32[1,1,80,13,128]{4,2,3,1,0:T(8,128)} fusion(f32[80,13,128]{2,0,1:T(8,128)S(1)} %fusion.14, f32[80,13,128]{2,0,1:T(8,128)S(1)} %convolution_add_fusion.1, f32[80,96,1]{0,1,2:T(8,128)S(1)} %bitcast.326, f32[12,13,8,128]{3,2,1,0:T(8,128)S(1)} %fusion.11), kind=kOutput, calls=%fused_computation.34 | convolution fusion | flops 153620480 | bytes 2267136 | tf_op jit(solution)/shard_map/dot_general | solution.py:62
  (197 shorter events, 29.5 us)
Async XLA Ops:
  0.6 31.7 %copy-start = (bf16[1,1,4,1024,128]{4,3,2,1,0:T(8,128)(2,1)S(1)}, bf16[1,1,4,1024,128]{4,3,2,1,0:T(8,128)(2,1)}, u32[]{:S(2)}) copy-start(bf16[1,1,4,1024,128]{4,3,2,1,0:T(8,128)(2,1)} %param.11) | copy-start | bytes 3145732
  0.6 11.9 %copy-start.12 = (bf16[1,1,80,1024]{3,2,1,0:T(8,128)(2,1)S(1)}, bf16[1,1,80,1024]{3,2,1,0:T(8,128)(2,1)}, u32[]{:S(2)}) copy-start(bf16[1,1,80,1024]{3,2,1,0:T(8,128)(2,1)} %param.10) | copy-start | bytes 491524
  0.7 11.1 %copy-start.1 = (s32[1,1,64]{2,1,0:T(1,128)S(1)}, s32[1,1,64]{2,1,0:T(1,128)}, u32[]{:S(2)}) copy-start(s32[1,1,64]{2,1,0:T(1,128)} %param.16) | copy-start | bytes 772
  0.7 11.9 %copy-start.24 = (s32[1,1,4]{2,1,0:T(1,128)S(1)}, s32[1,1,4]{2,1,0:T(1,128)}, u32[]{:S(2)}) copy-start(s32[1,1,4]{2,1,0:T(1,128)} %param.12) | copy-start | bytes 52
  0.7 11.9 %collective-permute-start = (bf16[1,1,80,1024]{3,2,1,0:T(8,128)(2,1)}, bf16[1,1,80,1024]{3,2,1,0:T(8,128)(2,1)S(1)}, u32[]{:S(2)}, u32[]{:S(2)}) collective-permute-start(bf16[1,1,80,1024]{3,2,1,0:T(8,128)(2,1)} %param.10), channel_id=1, source_target_pairs={{0,16},{16,32},{32,48},{48,64},{64,80},{80,96},{96,112},{1,17},{17... | collective-permute-start | bytes 491528 | tf_op jit(solution)/shard_map/ppermute | solution.py:26
  4.9 7.7 %collective-permute-start.1 = (bf16[1,1,80,1024]{3,2,1,0:T(8,128)(2,1)}, bf16[1,1,80,1024]{3,2,1,0:T(8,128)(2,1)S(1)}, u32[]{:S(2)}, u32[]{:S(2)}) collective-permute-start(bf16[1,1,80,1024]{3,2,1,0:T(8,128)(2,1)} %param.10), channel_id=1, source_target_pairs={{16,0},{32,16},{48,32},{64,48},{80,64},{96,80},{112,96},{17,1},{33... | collective-permute-start | bytes 491528 | tf_op jit(solution)/shard_map/ppermute | solution.py:29
  7.7 12.4 %copy-start.2 = (f32[1,1,64]{2,1,0:T(1,128)S(1)}, f32[1,1,64]{2,1,0:T(1,128)}, u32[]{:S(2)}) copy-start(f32[1,1,64]{2,1,0:T(1,128)} %param.14) | copy-start | bytes 772
  9.0 11.9 %copy-start.3 = (f32[1,1,64]{2,1,0:T(1,128)S(1)}, f32[1,1,64]{2,1,0:T(1,128)}, u32[]{:S(2)}) copy-start(f32[1,1,64]{2,1,0:T(1,128)} %param.15) | copy-start | bytes 772
  12.6 15.1 %collective-permute-start.2 = (bf16[3,1,80,1024]{3,2,1,0:T(8,128)(2,1)S(1)}, bf16[3,1,80,1024]{3,2,1,0:T(8,128)(2,1)S(1)}, u32[]{:S(2)}, u32[]{:S(2)}) collective-permute-start(bf16[3,1,80,1024]{3,2,1,0:T(8,128)(2,1)S(1)} %constant_dynamic-update-slice_fusion), channel_id=1, source_target_pairs={{0,1},{1,2},{2,3},{3,4},{4,5},{5,6},{6,7},{7,8},{8,9},{9,10},{10,1... | collective-permute-start | bytes 1474568 | tf_op jit(solution)/shard_map/ppermute | solution.py:26
  15.9 13.6 %collective-permute-start.3 = (bf16[3,1,80,1024]{3,2,1,0:T(8,128)(2,1)S(1)}, bf16[3,1,80,1024]{3,2,1,0:T(8,128)(2,1)S(1)}, u32[]{:S(2)}, u32[]{:S(2)}) collective-permute-start(bf16[3,1,80,1024]{3,2,1,0:T(8,128)(2,1)S(1)} %constant_dynamic-update-slice_fusion), channel_id=1, source_target_pairs={{1,0},{2,1},{3,2},{4,3},{5,4},{6,5},{7,6},{8,7},{9,8},{10,9},{11,1... | collective-permute-start | bytes 1474568 | tf_op jit(solution)/shard_map/ppermute | solution.py:29
  32.7 32.6 %copy-start.8 = (f32[80,1,128]{2,0,1:T(8,128)}, f32[80,1,128]{2,0,1:T(8,128)S(1)}, u32[]{:S(2)}) copy-start(f32[80,1,128]{2,0,1:T(8,128)S(1)} %convolution_bitcast_fusion) | copy-start | bytes 122884
  33.2 32.1 %copy-start.9 = (f32[13,128]{1,0:T(8,128)}, f32[13,128]{1,0:T(8,128)S(1)}, u32[]{:S(2)}) copy-start(f32[13,128]{1,0:T(8,128)S(1)} %broadcast_multiply_fusion) | copy-start | bytes 19972
  36.1 7.9 %collective-permute-start.4 = (f32[1,1,85,32]{2,3,1,0:T(8,128)S(1)}, f32[1,1,85,32]{2,3,1,0:T(8,128)S(1)}, u32[]{:S(2)}, u32[]{:S(2)}) collective-permute-start(f32[1,1,85,32]{2,3,1,0:T(8,128)S(1)} %bitcast.328), channel_id=1, source_target_pairs={{0,16},{16,32},{32,48},{48,64},{64,80},{80,96},{96,112},{1,17},{17... | collective-permute-start | bytes 32648 | tf_op jit(solution)/shard_map/ppermute | solution.py:26
  41.5 5.1 %collective-permute-start.5 = (f32[1,1,85,32]{2,3,1,0:T(8,128)S(1)}, f32[1,1,85,32]{2,3,1,0:T(8,128)S(1)}, u32[]{:S(2)}, u32[]{:S(2)}) collective-permute-start(f32[1,1,85,32]{2,3,1,0:T(8,128)S(1)} %bitcast.329), channel_id=1, source_target_pairs={{16,0},{32,16},{48,32},{64,48},{80,64},{96,80},{112,96},{17,1},{33... | collective-permute-start | bytes 32648 | tf_op jit(solution)/shard_map/ppermute | solution.py:29
  46.6 11.7 %collective-permute-start.6 = (f32[3,1,85,32]{2,3,1,0:T(8,128)S(1)}, f32[3,1,85,32]{2,3,1,0:T(8,128)S(1)}, u32[]{:S(2)}, u32[]{:S(2)}) collective-permute-start(f32[3,1,85,32]{2,3,1,0:T(8,128)S(1)} %pad_maximum_fusion.4), channel_id=1, source_target_pairs={{0,1},{1,2},{2,3},{3,4},{4,5},{5,6},{6,7},{7,8},{8,9},{9,10},{10,1... | collective-permute-start | bytes 97928 | tf_op jit(solution)/shard_map/ppermute | solution.py:26
  49.7 8.6 %collective-permute-start.7 = (f32[3,1,85,32]{2,3,1,0:T(8,128)S(1)}, f32[3,1,85,32]{2,3,1,0:T(8,128)S(1)}, u32[]{:S(2)}, u32[]{:S(2)}) collective-permute-start(f32[3,1,85,32]{2,3,1,0:T(8,128)S(1)} %pad_maximum_fusion.4), channel_id=1, source_target_pairs={{1,0},{2,1},{3,2},{4,3},{5,4},{6,5},{7,6},{8,7},{9,8},{10,9},{11,1... | collective-permute-start | bytes 97928 | tf_op jit(solution)/shard_map/ppermute | solution.py:29
  54.9 8.5 %copy-start.20 = (f32[128]{0:T(128)}, f32[128]{0:T(128)S(1)}, u32[]{:S(2)}) copy-start(f32[128]{0:T(128)S(1)} %get-tuple-element.70) | copy-start | bytes 1540
  54.9 8.5 %copy-start.22 = (f32[128]{0:T(128)}, f32[128]{0:T(128)S(1)}, u32[]{:S(2)}) copy-start(f32[128]{0:T(128)S(1)} %get-tuple-element.71) | copy-start | bytes 1540
  66.2 2.4 %copy-start.7 = (f32[80,13,128]{2,0,1:T(8,128)S(1)}, f32[80,13,128]{2,0,1:T(8,128)}, u32[]{:S(2)}) copy-start(f32[80,13,128]{2,0,1:T(8,128)} %copy-done.6) | copy-start | bytes 1597444
  66.2 2.4 %copy-start.11 = (f32[80,3,32]{0,2,1:T(8,128)S(1)}, f32[80,3,32]{0,2,1:T(8,128)}, u32[]{:S(2)}) copy-start(f32[80,3,32]{0,2,1:T(8,128)} %bitcast_multiply_fusion.7) | copy-start | bytes 92164
  68.6 3.2 %copy-start.19 = (f32[3,32]{1,0:T(4,128)S(1)}, f32[3,32]{1,0:T(4,128)}, u32[]{:S(2)}) copy-start(f32[3,32]{1,0:T(4,128)} %get-tuple-element.31) | copy-start | bytes 1156
  69.2 3.6 %copy-start.14 = (f32[13,128]{1,0:T(8,128)S(1)}, f32[13,128]{1,0:T(8,128)}, u32[]{:S(2)}) copy-start(f32[13,128]{1,0:T(8,128)} %copy-done.13) | copy-start | bytes 19972
  70.0 5.9 %copy-start.15 = (f32[1,32]{0,1:T(8,128)S(1)}, f32[1,32]{0,1:T(8,128)}, u32[]{:S(2)}) copy-start(f32[1,32]{0,1:T(8,128)} %get-tuple-element.44) | copy-start | bytes 388
  70.0 5.9 %copy-start.16 = (f32[1,32]{0,1:T(8,128)S(1)}, f32[1,32]{0,1:T(8,128)}, u32[]{:S(2)}) copy-start(f32[1,32]{0,1:T(8,128)} %get-tuple-element.45) | copy-start | bytes 388
  71.8 4.1 %copy-start.17 = (f32[1,32]{0,1:T(8,128)S(1)}, f32[1,32]{0,1:T(8,128)}, u32[]{:S(2)}) copy-start(f32[1,32]{0,1:T(8,128)} %copy.62) | copy-start | bytes 388
  71.8 4.1 %copy-start.18 = (f32[1,32]{0,1:T(8,128)S(1)}, f32[1,32]{0,1:T(8,128)}, u32[]{:S(2)}) copy-start(f32[1,32]{0,1:T(8,128)} %copy.61) | copy-start | bytes 388
  73.5 21.1 %copy-start.21 = (f32[128]{0:T(128)S(1)}, f32[128]{0:T(128)}, u32[]{:S(2)}) copy-start(f32[128]{0:T(128)} %copy-done.20) | copy-start | bytes 1540
  73.6 21.1 %copy-start.23 = (f32[128]{0:T(128)S(1)}, f32[128]{0:T(128)}, u32[]{:S(2)}) copy-start(f32[128]{0:T(128)} %copy-done.22) | copy-start | bytes 1540
  76.0 4.3 %collective-permute-start.8 = (f32[1,1,85,32]{2,3,1,0:T(8,128)S(1)}, f32[1,1,85,32]{2,3,1,0:T(8,128)S(1)}, u32[]{:S(2)}, u32[]{:S(2)}) collective-permute-start(f32[1,1,85,32]{2,3,1,0:T(8,128)S(1)} %bitcast.332), channel_id=1, source_target_pairs={{0,16},{16,32},{32,48},{48,64},{64,80},{80,96},{96,112},{1,17},{17... | collective-permute-start | bytes 32648 | tf_op jit(solution)/shard_map/ppermute | solution.py:26
  78.2 5.1 %collective-permute-start.9 = (f32[1,1,85,32]{2,3,1,0:T(8,128)S(1)}, f32[1,1,85,32]{2,3,1,0:T(8,128)S(1)}, u32[]{:S(2)}, u32[]{:S(2)}) collective-permute-start(f32[1,1,85,32]{2,3,1,0:T(8,128)S(1)} %bitcast.333), channel_id=1, source_target_pairs={{16,0},{32,16},{48,32},{64,48},{80,64},{96,80},{112,96},{17,1},{33... | collective-permute-start | bytes 32648 | tf_op jit(solution)/shard_map/ppermute | solution.py:29
  83.2 7.6 %collective-permute-start.10 = (f32[3,1,85,32]{2,3,1,0:T(8,128)S(1)}, f32[3,1,85,32]{2,3,1,0:T(8,128)S(1)}, u32[]{:S(2)}, u32[]{:S(2)}) collective-permute-start(f32[3,1,85,32]{2,3,1,0:T(8,128)S(1)} %pad_maximum_fusion.5), channel_id=1, source_target_pairs={{0,1},{1,2},{2,3},{3,4},{4,5},{5,6},{6,7},{7,8},{8,9},{9,10},{10,1... | collective-permute-start | bytes 97928 | tf_op jit(solution)/shard_map/ppermute | solution.py:26
  85.2 6.6 %collective-permute-start.11 = (f32[3,1,85,32]{2,3,1,0:T(8,128)S(1)}, f32[3,1,85,32]{2,3,1,0:T(8,128)S(1)}, u32[]{:S(2)}, u32[]{:S(2)}) collective-permute-start(f32[3,1,85,32]{2,3,1,0:T(8,128)S(1)} %pad_maximum_fusion.5), channel_id=1, source_target_pairs={{1,0},{2,1},{3,2},{4,3},{5,4},{6,5},{7,6},{8,7},{9,8},{10,9},{11,1... | collective-permute-start | bytes 97928 | tf_op jit(solution)/shard_map/ppermute | solution.py:29
  (5 other events, 6.0 us)
where the time goes:
time: 104 us; the launch traced here: 102 us
  starting transfers between devices  41.1 us (40%)
  local copies, waits for them, and re-layouts  22.4 us (22%)
  matrix products  14.5 us (14%)
  waiting for transfers between devices  13.4 us (13%)
  other arithmetic  9.46 us (9%)
  between operations  1.53 us (1%)
    ppermute x6, starting transfers between devices, extended(): lax.ppermute(lax.slice_in_dim(block, 0, width, axis=dim), axis, backward)  21 us
    ppermute x6, starting transfers between devices, extended(): lax.ppermute(lax.slice_in_dim(block, block.shape[dim] - width, None, axis...  20.1 us
    ppermute x6, waiting for transfers between devices, extended(): lax.ppermute(lax.slice_in_dim(block, 0, width, axis=dim), axis, backward)  8.14 us
    dot_general x6, matrix products, update_group(): jnp.dot(observed.T, flat_anomaly, precision=exact_mode, preferred_element...  5.78 us
    ppermute x6, waiting for transfers between devices, extended(): lax.ppermute(lax.slice_in_dim(block, block.shape[dim] - width, None, axis...  5.26 us
    dot_general x6, matrix products, update_group(): jnp.dot(observed * damping[None, :], gain, precision=exact_mode, preferre...  4.66 us
    unnamed x55, local copies, waits for them, and re-layouts  3.86 us
    dot_general x6, matrix products, update_group(): jnp.dot(innovation[None, :], gain, precision=exact_mode, preferred_elemen...  3.1 us
  transfers between devices with their start and end apart: 12, of which 5 were waited for; matrix products, arithmetic and copies ran while one was open for 12% of the time, Pallas kernels for 0%

commit v1 on v0

v1 whole, which is shorter than its diff:
```python
import functools

import jax
import jax.numpy as jnp
from jax import lax
from jax.experimental import pallas as pl
from jax.experimental.pallas import tpu as pltpu
from jax.sharding import PartitionSpec as P

MEM = 80
AX = 8
AY = 16
OCN_DEV = 1024
OB = 32
NB = 2
K = 4
FIELDS = 12
COMP = 13
CELLS = 128
OBS = 64
ROWS = 88
GROUPS = 11
CHUNKS = 4
CW = OCN_DEV // CHUNKS

MESH = pl.DeviceIdType.MESH
NEAR = [(dx, dy) for dx in (-1, 0, 1) for dy in (-1, 0, 1)]
AROUND = [d for d in NEAR if d != (0, 0)]


def slot(dx, dy):
    return (dx + 1) * 3 + dy + 1


def roll(x, shift):
    shift = shift % CELLS
    return x if shift == 0 else pltpu.roll(x, shift, 1)


def exchange_kernel(
    src,
    ocean,
    weights,
    cell,
    value,
    error,
    live,
    order,
    f_out,
    meta_out,
    oce,
    wv,
    acc,
    meta,
    meta_in,
    pack_y,
    pack_x,
    in_w,
    in_e,
    in_n,
    in_s,
    local_sem,
    oce_send,
    oce_recv,
    relay_send,
    meta_send,
    meta_recv,
    halo_send,
    halo_recv,
):
    i = lax.axis_index("gx")
    j = lax.axis_index("gy")
    nx = lax.axis_size("gx")
    ny = lax.axis_size("gy")

    def has(dx, dy):
        cond = None
        for pos, step, count in ((i, dx, nx), (j, dy, ny)):
            if step:
                ok = (pos > 0) if step < 0 else (pos < count - 1)
                cond = ok if cond is None else jnp.logical_and(cond, ok)
        return cond

    def when(dx, dy):
        return pl.when(has(dx, dy))

    def device(dx, dy):
        return (i + dx, j + dy)

    barrier = pltpu.get_barrier_semaphore()
    for dx, dy in AROUND:

        @when(dx, dy)
        def _():
            pl.semaphore_signal(
                barrier, inc=1, device_id=device(dx, dy), device_id_type=MESH
            )

    own_load = [
        pltpu.make_async_copy(
            ocean.at[:, pl.ds(c * CW, CW)], oce.at[4, c], local_sem.at[c]
        )
        for c in range(CHUNKS)
    ]
    for copy in own_load:
        copy.start()
    w_load = pltpu.make_async_copy(weights, wv, local_sem.at[CHUNKS])
    w_load.start()

    lane = lax.broadcasted_iota(jnp.int32, (OBS, OBS), 0)
    perm = jnp.where(lane == order[...], 1.0, 0.0)
    rows = [
        cell[...].astype(jnp.float32),
        value[...],
        error[...],
        live[...].astype(jnp.float32),
    ]
    stacked = jnp.concatenate(rows + [jnp.zeros((4, OBS), jnp.float32)], axis=0)
    ordered = jnp.dot(
        stacked,
        perm,
        precision=lax.Precision.HIGHEST,
        preferred_element_type=jnp.float32,
    )
    meta[...] = jnp.concatenate([ordered, jnp.zeros((8, CELLS - OBS), jnp.float32)], axis=1)

    xs = 1 + jnp.where(jnp.logical_and(i > 0, i < nx - 1), 1, 0)
    ys = 1 + jnp.where(jnp.logical_and(j > 0, j < ny - 1), 1, 0)
    pl.semaphore_wait(barrier, (xs + 1) * (ys + 1) - 1)

    def ocean_copy(c, dx, dy):
        return pltpu.make_async_remote_copy(
            src_ref=oce.at[4, c],
            dst_ref=oce.at[slot(-dx, -dy), c],
            send_sem=oce_send.at[slot(dx, dy), c],
            recv_sem=oce_recv.at[slot(-dx, -dy), c],
            device_id=device(dx, dy),
            device_id_type=MESH,
        )

    def relay_copy(c, dx, dy):
        return pltpu.make_async_remote_copy(
            src_ref=oce.at[slot(0, dy), c],
            dst_ref=oce.at[slot(-dx, dy), c],
            send_sem=relay_send.at[slot(dx, dy), c],
            recv_sem=oce_recv.at[slot(-dx, dy), c],
            device_id=device(dx, 0),
            device_id_type=MESH,
        )

    def meta_copy(dx, dy):
        return pltpu.make_async_remote_copy(
            src_ref=meta,
            dst_ref=meta_in.at[slot(-dx, -dy)],
            send_sem=meta_send.at[slot(dx, dy)],
            recv_sem=meta_recv.at[slot(-dx, -dy)],
            device_id=device(dx, dy),
            device_id_type=MESH,
        )

    for c in range(CHUNKS):
        own_load[c].wait()
        for dx, dy in ((0, -1), (0, 1), (-1, 0), (1, 0)):

            @when(dx, dy)
            def _():
                ocean_copy(c, dx, dy).start()

    for dx, dy in AROUND:

        @when(dx, dy)
        def _():
            meta_copy(dx, dy).start()

    positions = [
        (src[0, k] // ny - i + 1) * 3 + (src[0, k] % ny - j + 1) for k in range(K)
    ]

    def product(p, c):
        which = jnp.int32(0)
        valid = positions[0] == p
        for k in range(1, K):
            which = jnp.where(positions[k] == p, k, which)
            valid = jnp.logical_or(valid, positions[k] == p)
        part = jnp.dot(
            oce[p, c],
            wv[which, pl.ds(c * CW, CW), :],
            preferred_element_type=jnp.float32,
        )
        return jnp.where(valid, part, 0.0)

    w_load.wait()
    total = product(4, 0)
    for c in range(1, CHUNKS):
        total = total + product(4, c)
    acc[...] = total

    for c in range(CHUNKS):
        for dy in (-1, 1):

            @when(0, dy)
            def _():
                ocean_copy(c, 0, -dy).wait_recv()
                for dx in (-1, 1):

                    @when(dx, 0)
                    def _():
                        relay_copy(c, dx, dy).start()

        for dx, dy in ((-1, 0), (1, 0)):

            @when(dx, dy)
            def _():
                ocean_copy(c, -dx, -dy).wait_recv()
                acc[...] += product(slot(dx, dy), c)

        for dx, dy in ((0, -1), (0, 1)):

            @when(dx, dy)
            def _():
                acc[...] += product(slot(dx, dy), c)

    for dx, dy in AROUND:

        @when(dx, dy)
        def _():
            meta_copy(-dx, -dy).wait_recv()

    blocks = []
    for dx, dy in NEAR:
        if (dx, dy) == (0, 0):
            blocks.append(meta[...])
        else:
            blocks.append(jnp.where(has(dx, dy), meta_in[slot(dx, dy)], 0.0))
    blocks.append(jnp.zeros((CELLS - 72, CELLS), jnp.float32))
    columns = jnp.concatenate(blocks, axis=0).T
    meta_out[...] = columns[:OBS, :]

    for c in range(CHUNKS):
        for dx, dy in ((-1, -1), (-1, 1), (1, -1), (1, 1)):

            @when(dx, dy)
            def _():
                relay_copy(c, -dx, dy).wait_recv()
                acc[...] += product(slot(dx, dy), c)

    sst = acc[...]
    mean = jnp.sum(sst, axis=0, keepdims=True) / MEM
    anomaly = sst - mean
    pieces = [anomaly[8 * g : 8 * g + 8] for g in range(MEM // 8)]
    head = lax.broadcasted_iota(jnp.int32, (8, CELLS), 0) == 0
    pieces.append(jnp.where(head, mean, 0.0))
    lane8 = lax.broadcasted_iota(jnp.int32, (8, CELLS), 1)
    pair = (lane8 % AY) // 2
    quarter = lane8 // 32

    for block in range(2):
        west = jnp.zeros((8, CELLS), jnp.float32)
        east = west
        for g in range(8 * block, min(8 * block + 8, GROUPS)):
            s = g % 8
            west = jnp.where(pair == s, roll(pieces[g], 2 * s), west)
            east = jnp.where(pair == 7 - s, roll(pieces[g], -2 * s), east)
        pack_y[0, 8 * block : 8 * block + 8, :] = west
        pack_y[1, 8 * block : 8 * block + 8, :] = east
    for block in range(3):
        north = jnp.zeros((8, CELLS), jnp.float32)
        south = north
        for g in range(4 * block, min(4 * block + 4, GROUPS)):
            s = g % 4
            north = jnp.where(quarter == s, roll(pieces[g], 32 * s), north)
            south = jnp.where(quarter == 3 - s, roll(pieces[g], -32 * s), south)
        pack_x[0, 8 * block : 8 * block + 8, :] = north
        pack_x[1, 8 * block : 8 * block + 8, :] = south

    def halo_copy(dx, dy):
        if dy < 0:
            source, target = pack_y.at[0], in_w.at[1 - dx]
        elif dy > 0:
            source, target = pack_y.at[1], in_e.at[1 - dx]
        elif dx < 0:
            source, target = pack_x.at[0], in_n
        else:
            source, target = pack_x.at[1], in_s
        return pltpu.make_async_remote_copy(
            src_ref=source,
            dst_ref=target,
            send_sem=halo_send.at[slot(dx, dy)],
            recv_sem=halo_recv.at[slot(-dx, -dy)],
            device_id=device(dx, dy),
            device_id_type=MESH,
        )

    f_out[0, :MEM, :] = anomaly
    f_out[0, MEM:, :] = pieces[-1]

    for dx, dy in AROUND[::-1]:

        @when(dx, dy)
        def _():
            halo_copy(dx, dy).start()

    for c in range(CHUNKS):
        for dx, dy in ((0, -1), (0, 1), (-1, 0), (1, 0)):

            @when(dx, dy)
            def _():
                ocean_copy(c, dx, dy).wait_send()

        for dy in (-1, 1):
            for dx in (-1, 1):

                @when(dx, dy)
                def _():
                    relay_copy(c, dx, dy).wait_send()

    for dx, dy in AROUND:

        @when(dx, dy)
        def _():
            meta_copy(dx, dy).wait_send()

    for dx, dy in AROUND:

        @when(dx, dy)
        def _():
            halo_copy(-dx, -dy).wait_recv()

    low_y = (lane8 % AY) < 8
    low_x = lane8 < 64
    zero = jnp.zeros((8, CELLS), jnp.float32)

    def present(ref, dx, dy):
        return jnp.where(has(dx, dy), ref[...], 0.0)

    north = present(in_n, 1, 0)
    south = present(in_s, -1, 0)
    west = present(in_w.at[1], 0, 1)
    east = present(in_e.at[1], 0, -1)
    low16 = lax.broadcasted_iota(jnp.int32, (16, CELLS), 1) < 64
    west_c = jnp.where(low16, present(in_w.at[2], 1, 1), present(in_w.at[0], -1, 1))
    east_c = jnp.where(low16, present(in_e.at[2], 1, -1), present(in_e.at[0], -1, -1))
    for g in range(GROUPS):
        at = pl.ds(8 * g, 8)
        b, s = g // 4, g % 4
        f_out[1, at, :] = jnp.where(
            low_x,
            roll(north[8 * b : 8 * b + 8], -32 * s),
            roll(south[8 * b : 8 * b + 8], 32 * s),
        )
        b, s = g // 8, g % 8
        for place, w, e in ((2, west, east), (3, west_c, east_c)):
            f_out[place, at, :] = jnp.where(
                low_y,
                roll(w[8 * b : 8 * b + 8], -2 * s),
                roll(e[8 * b : 8 * b + 8], 2 * s),
            )

    for dx, dy in AROUND:

        @when(dx, dy)
        def _():
            halo_copy(dx, dy).wait_send()


def update_kernel(
    f_in, meta, atm, mean_out, anom_out, state, fields, shifted, scaled, sst_mean
):
    lane8 = lax.broadcasted_iota(jnp.int32, (8, CELLS), 1)
    y8 = lane8 % AY
    first_y, last_y = y8 == 0, y8 == AY - 1
    first_x, last_x = lane8 < AY, lane8 >= CELLS - AY

    def shift_all(blocks, wanted):
        out = {}
        turned = {}
        for f in range(4):
            if any((f ^ a) in wanted for a in (0, 1)):
                other = blocks[f ^ 2]
                turned[f, 0] = blocks[f]
                turned[f, 1] = jnp.where(last_y, roll(other, 15), roll(blocks[f], -1))
                turned[f, -1] = jnp.where(first_y, roll(other, -15), roll(blocks[f], 1))
        for f in wanted:
            for dy in (-1, 0, 1):
                own, other = turned[f, dy], turned[f ^ 1, dy]
                out[f, 0, dy] = own
                out[f, 1, dy] = roll(jnp.where(first_x, other, own), -AY)
                out[f, -1, dy] = roll(jnp.where(last_x, other, own), AY)
        return out

    total = jnp.zeros((FIELDS, CELLS), jnp.float32)

    def add_member(m, total):
        return total + atm[m]

    total = lax.fori_loop(0, MEM, add_member, total, unroll=8)
    field_mean = total / MEM

    def put_member(m, carry):
        fields[m, :FIELDS, :] = atm[m] - field_mean
        fields[m, FIELDS:COMP, :] = f_in[0, pl.ds(m, 1), :]
        return carry

    lax.fori_loop(0, MEM, put_member, 0, unroll=8)
    fields[MEM, :FIELDS, :] = field_mean
    fields[MEM, FIELDS:COMP, :] = f_in[0, MEM : MEM + 1, :]

    row32 = lax.broadcasted_iota(jnp.int32, (OB, CELLS), 1)
    row1 = lax.broadcasted_iota(jnp.int32, (1, CELLS), 1)
    low_y1 = (row1 % AY) < 8
    low_x1 = row1 < 64

    for batch in range(NB):
        source = f_in if batch == 0 else state
        wanted = (0, 1, 2, 3) if batch == 0 else (0,)

        variance = [
            jnp.sum(source[f, :MEM, :] * source[f, :MEM, :], axis=0, keepdims=True)
            / (MEM - 1)
            for f in range(4)
        ]

        def observations(f, dx, dy):
            at = 8 * slot(dx, dy)
            rows = slice(batch * OB, (batch + 1) * OB)
            cells = meta[rows, at : at + 1]
            values = meta[rows, at + 1 : at + 2]
            errors = meta[rows, at + 2 : at + 3]
            alive = meta[rows, at + 3 : at + 4]
            denominator = variance[f] + errors + (1.0 - alive)
            weighting = alive / denominator
            damping = 1.0 / (1.0 + jnp.sqrt(errors / denominator))
            weighting = jnp.where(cells == row32.astype(jnp.float32), weighting, 0.0)
            innovation = values - source[f, MEM : MEM + 1, :]
            alpha = jnp.sum(weighting * innovation, axis=0, keepdims=True)
            beta = jnp.sum(weighting * damping, axis=0, keepdims=True)
            return jnp.concatenate([beta, alpha], axis=0)

        pick = jnp.where
        sums = [
            observations(0, 0, 0),
            pick(low_x1, observations(1, 1, 0), observations(1, -1, 0)),
            pick(low_y1, observations(2, 0, 1), observations(2, 0, -1)),
            pick(
                low_y1,
                pick(low_x1, observations(3, 1, 1), observations(3, -1, 1)),
                pick(low_x1, observations(3, 1, -1), observations(3, -1, -1)),
            ),
        ]
        pad = jnp.zeros((6, CELLS), jnp.float32)
        factors = shift_all([jnp.concatenate([s, pad], axis=0) for s in sums], wanted)

        for g in range(MEM // 8):
            at = slice(8 * g, 8 * g + 8)
            moved = shift_all([source[f, at, :] for f in range(4)], wanted)
            for f in wanted:
                for dx, dy in NEAR:
                    shifted[f, slot(dx, dy), at, :] = moved[f, dx, dy]

        def taper(dx, dy):
            return max(1.0 - (dx * dx + dy * dy) / 4.0, 0.0) ** 2 / (MEM - 1)

        if batch + 1 < NB:
            for f in wanted:
                own = source[f, :MEM, :]
                new = own
                mean = source[f, MEM : MEM + 1, :]
                for dx, dy in NEAR:
                    h = shifted[f, slot(dx, dy), :MEM, :]
                    gain = jnp.sum(h * own, axis=0, keepdims=True) * taper(dx, dy)
                    beta = factors[f, dx, dy][0:1]
                    alpha = factors[f, dx, dy][1:2]
                    new = new - h * (beta * gain)
                    mean = mean + alpha * gain
                state[f, :MEM, :] = new
                state[f, MEM : MEM + 1, :] = mean

        for dx, dy in NEAR:
            d = slot(dx, dy)
            beta = factors[0, dx, dy][0:1]
            scaled[d, :MEM, :] = shifted[0, d, :MEM, :] * beta
            scaled[d, MEM : MEM + 1, :] = -factors[0, dx, dy][1:2]

        def accumulate(m, sums):
            block = fields[m]
            return tuple(
                s + shifted[0, d, pl.ds(m, 1), :] * block for d, s in enumerate(sums)
            )

        gains = lax.fori_loop(
            0,
            MEM,
            accumulate,
            tuple(jnp.zeros((COMP, CELLS), jnp.float32) for _ in NEAR),
            unroll=8,
        )
        gains = [g * taper(dx, dy) for g, (dx, dy) in zip(gains, NEAR)]

        def updated(m):
            block = fields[m]
            for d, gain in enumerate(gains):
                block = block - scaled[d, pl.ds(m, 1), :] * gain
            return block

        def apply(m, carry):
            if batch + 1 < NB:
                fields[m] = updated(m)
            else:
                anom_out[m] = updated(m)
            return carry

        lax.fori_loop(0, MEM, apply, 0, unroll=8)
        if batch + 1 < NB:
            fields[MEM] = updated(MEM)
        else:
            mean_out[...] = updated(MEM)


def local(
    atm_members,
    ocean_members,
    remap_weights,
    pair_src,
    obs_cell,
    obs_value,
    obs_error,
    obs_live,
    obs_order,
):
    f32 = jnp.float32
    vmem = pl.BlockSpec(memory_space=pltpu.VMEM)
    anywhere = pl.BlockSpec(memory_space=pl.ANY)
    dma = pltpu.SemaphoreType.DMA
    state, meta = pl.pallas_call(
        exchange_kernel,
        out_shape=(
            jax.ShapeDtypeStruct((4, ROWS, CELLS), f32),
            jax.ShapeDtypeStruct((OBS, CELLS), f32),
        ),
        in_specs=[pl.BlockSpec(memory_space=pltpu.SMEM), anywhere, anywhere] + [vmem] * 5,
        out_specs=(vmem, vmem),
        scratch_shapes=[
            pltpu.VMEM((9, CHUNKS, MEM, CW), jnp.bfloat16),
            pltpu.VMEM((K, OCN_DEV, CELLS), jnp.bfloat16),
            pltpu.VMEM((MEM, CELLS), f32),
            pltpu.VMEM((8, CELLS), f32),
            pltpu.VMEM((9, 8, CELLS), f32),
            pltpu.VMEM((2, 16, CELLS), f32),
            pltpu.VMEM((2, 24, CELLS), f32),
            pltpu.VMEM((3, 16, CELLS), f32),
            pltpu.VMEM((3, 16, CELLS), f32),
            pltpu.VMEM((24, CELLS), f32),
            pltpu.VMEM((24, CELLS), f32),
            dma((CHUNKS + 1,)),
            dma((9, CHUNKS)),
            dma((9, CHUNKS)),
            dma((9, CHUNKS)),
            dma((9,)),
            dma((9,)),
            dma((9,)),
            dma((9,)),
        ],
        compiler_params=pltpu.CompilerParams(
            collective_id=0, has_side_effects=True, vmem_limit_bytes=16 * 1024 * 1024
        ),
    )(
        pair_src[0],
        ocean_members[0, 0],
        remap_weights[0, 0],
        obs_cell[0],
        obs_value[0],
        obs_error[0],
        obs_live[0],
        obs_order[0],
    )
    mean, anomaly = pl.pallas_call(
        update_kernel,
        out_shape=(
            jax.ShapeDtypeStruct((COMP, CELLS), f32),
            jax.ShapeDtypeStruct((MEM, COMP, CELLS), f32),
        ),
        in_specs=[vmem] * 3,
        out_specs=(vmem, vmem),
        scratch_shapes=[
            pltpu.VMEM((4, ROWS, CELLS), f32),
            pltpu.VMEM((MEM + 1, COMP, CELLS), f32),
            pltpu.VMEM((4, 9, MEM, CELLS), f32),
            pltpu.VMEM((9, ROWS, CELLS), f32),
            pltpu.VMEM((8, CELLS), f32),
        ],
        compiler_params=pltpu.CompilerParams(vmem_limit_bytes=16 * 1024 * 1024),
    )(state, meta, atm_members[0, 0])
    return (mean[None, None], anomaly[None, None])


def solution(mesh):
    in_specs = (
        P("gx", "gy", None, None, None),
        P("gx", "gy", None, None),
        P("gx", "gy", None, None, None),
        P("gx", "gy", None),
        P("gx", "gy", None),
        P("gx", "gy", None),
        P("gx", "gy", None),
        P("gx", "gy", None),
        P("gx", "gy", None),
    )
    out_specs = (P("gx", "gy", None, None), P("gx", "gy", None, None, None))
    return jax.shard_map(local, mesh=mesh, in_specs=in_specs, out_specs=out_specs, check_vma=False)
```

time: 104 us -> 31.1 us (0.30); the launches traced: 102 us -> 30.9 us
  starting transfers between devices: 41.1 us -> 0 us
  Pallas kernels: 0 us -> 25.7 us
  local copies, waits for them, and re-layouts: 22.4 us -> 4.56 us
  matrix products: 14.5 us -> 0 us
  waiting for transfers between devices: 13.4 us -> 0 us
  other arithmetic: 9.46 us -> 0 us
    ppermute x12 -> x0, starting transfers between devices: 41.1 us -> none  [the longest x6 21 us: extended(): lax.ppermute(lax.slice_in_dim(block, 0, width, axis=dim), axis, backward)]
    pallas_call x0 -> x2, Pallas kernels: none -> 25.7 us  [the longest x1 20.9 us: local(): pl.pallas_call(exchange_kernel, out_shape=(jax.ShapeDtypeStruct((4, ROWS,...]
    dot_general x20 -> x0, matrix products: 14.5 us -> none  [the longest x6 5.78 us: update_group(): jnp.dot(observed.T, flat_anomaly, precision=exact_mode, preferred_element...]
    ppermute x12 -> x0, waiting for transfers between devices: 13.4 us -> none  [the longest x6 8.14 us: extended(): lax.ppermute(lax.slice_in_dim(block, 0, width, axis=dim), axis, backward)]
    gather x14 -> x0, local copies, waits for them, and re-layouts: 11.1 us -> none  [the longest x4 2.9 us: local(): obs_cells = obs_cell[0, 0][obs_slots]]
    sub x9 -> x0, other arithmetic: 3.58 us -> none  [the longest x6 2.85 us: update_group(): denominator = variance + errors + (1.0 - live)]
    another operation x19 -> x0, local copies, waits for them, and re-layouts: 2.17 us -> none  [the longest x2 0.78 us: local(): extras = jnp.stack([innovation, errors, pos_x, pos_y, live], axis=0)]
    mul x8 -> x0, other arithmetic: 2.1 us -> none  [the longest x6 1.73 us: update_group(): observed * damping[None, :]]
  transfers between devices with their start and end apart: 12 -> 0, of which waited for: 5 -> 0; matrix products, arithmetic and copies ran while one was open for 12% -> 0% of each run, Pallas kernels for 0% -> 0%
where the time goes in v1:
time: 31.1 us; the launch traced here: 30.9 us
  Pallas kernels  25.7 us (83%)
  local copies, waits for them, and re-layouts  4.56 us (15%)
  between operations  0.71 us (2%)
    pallas_call x1, Pallas kernels, local(): pl.pallas_call(exchange_kernel, out_shape=(jax.ShapeDtypeStruct((4, ROWS,...  20.9 us
    pallas_call x1, Pallas kernels, local(): pl.pallas_call(update_kernel, out_shape=(jax.ShapeDtypeStruct((COMP, CELL...  4.75 us
    unnamed x21, local copies, waits for them, and re-layouts  4.56 us

profile of v1, /device:TPU:7, one launch (start us, length us, event | category | flops | bytes accessed | tf_op | source)
XLA Modules:
  0.0 30.9 jit_solution(5282181329488372536)
XLA Ops:
  0.6 0.0 copy-start.5
  0.6 0.0 copy-start.6
  0.7 0.0 copy-start.7
  0.7 0.0 copy-start.2
  0.7 0.0 copy-start.3
  0.7 0.0 copy-start.4
  0.7 0.6 %copy-done.5 = f32[1,1,64]{2,1,0:T(1,128)S(1)} copy-done((f32[1,1,64]{2,1,0:T(1,128)S(1)}, f32[1,1,64]{2,1,0:T(1,128)}, u32[]{:S(2)}) %copy-start.5) | copy-done | bytes 280
  1.3 0.0 copy-done.6
  1.3 0.0 copy-done.7
  1.3 0.0 copy-done.2
  1.3 0.0 copy-done.3
  1.4 0.0 copy-done.4
  1.4 0.0 copy-start
  1.4 1.2 %copy-done = bf16[1,1,4,1024,128]{4,3,2,1,0:T(8,128)(2,1)S(1)} copy-done((bf16[1,1,4,1024,128]{4,3,2,1,0:T(8,128)(2,1)S(1)}, bf16[1,1,4,1024,128]{4,3,2,1,0:T(8,128)(2,1)}, u32[]{:S(2)}) %copy-start) | copy-done | bytes 1048600
  2.6 0.0 copy-start.1
  2.6 0.9 %copy-done.1 = bf16[1,1,80,1024]{3,2,1,0:T(8,128)(2,1)S(1)} copy-done((bf16[1,1,80,1024]{3,2,1,0:T(8,128)(2,1)S(1)}, bf16[1,1,80,1024]{3,2,1,0:T(8,128)(2,1)}, u32[]{:S(2)}) %copy-start.1) | copy-done | bytes 163864
  3.5 0.0 copy-start.8
  3.5 20.9 %shard_map.104 = (f32[4,88,128]{2,1,0:T(8,128)S(1)}, f32[64,128]{1,0:T(8,128)S(1)}) custom-call(s32[1,4]{1,0:T(1,128)S(1)} %bitcast.18, bf16[80,1024]{1,0:T(8,128)(2,1)S(1)} %bitcast.16, bf16[4,1024,128]{2,1,0:T(8,128)(2,1)S(1)} %bitcast.14, s32[1,64]{1,0:T(1,128)S(1)} %bitcast.19, f32[1,64]{1,0:T(1,128)S(1)} %bitcast.20, f32[1,64]{1,0:T(1,128)S(1)} %bitcast.21, ...), custom_call_target="tpu_custom_call" | custom-call | tf_op jit(solution)/shard_map/pallas_call | solution.py:534
  24.4 0.0 copy-done.8
  24.4 0.2 copy.15
  24.6 4.8 %shard_map.105 = (f32[13,128]{1,0:T(8,128)S(1)}, f32[80,13,128]{2,1,0:T(8,128)S(1)}) custom-call(f32[4,88,128]{2,1,0:T(8,128)S(1)} %get-tuple-element.6.f_in, f32[64,128]{1,0:T(8,128)S(1)} %get-tuple-element.7.meta, f32[80,12,128]{2,1,0:T(8,128)S(1)} %bitcast.13), custom_call_target="tpu_custom_call" | custom-call | tf_op jit(solution)/shard_map/pallas_call | solution.py:576
  29.4 0.6 %copy.12 = f32[1,1,13,128]{3,1,2,0:T(1,128)} copy(f32[1,1,13,128]{3,2,1,0:T(8,128)S(1)} %bitcast.17) | data formatting | bytes 13312
  30.0 1.0 %copy.13 = f32[1,1,80,13,128]{4,2,3,1,0:T(8,128)} copy(f32[1,1,80,13,128]{4,3,2,1,0:T(8,128)S(1)} %bitcast.15) | data formatting | bytes 1064960
Async XLA Ops:
  0.6 0.7 %copy-start.5 = (f32[1,1,64]{2,1,0:T(1,128)S(1)}, f32[1,1,64]{2,1,0:T(1,128)}, u32[]{:S(2)}) copy-start(f32[1,1,64]{2,1,0:T(1,128)} %param.15) | copy-start | bytes 772
  0.6 0.7 %copy-start.6 = (s32[1,1,64]{2,1,0:T(1,128)S(1)}, s32[1,1,64]{2,1,0:T(1,128)}, u32[]{:S(2)}) copy-start(s32[1,1,64]{2,1,0:T(1,128)} %param.16) | copy-start | bytes 772
  0.7 0.7 %copy-start.7 = (s32[1,1,64]{2,1,0:T(1,128)S(1)}, s32[1,1,64]{2,1,0:T(1,128)}, u32[]{:S(2)}) copy-start(s32[1,1,64]{2,1,0:T(1,128)} %param.17) | copy-start | bytes 772
  0.7 0.7 %copy-start.2 = (s32[1,1,4]{2,1,0:T(1,128)S(1)}, s32[1,1,4]{2,1,0:T(1,128)}, u32[]{:S(2)}) copy-start(s32[1,1,4]{2,1,0:T(1,128)} %param.12) | copy-start | bytes 52
  0.7 0.7 %copy-start.3 = (s32[1,1,64]{2,1,0:T(1,128)S(1)}, s32[1,1,64]{2,1,0:T(1,128)}, u32[]{:S(2)}) copy-start(s32[1,1,64]{2,1,0:T(1,128)} %param.13) | copy-start | bytes 772
  0.7 0.7 %copy-start.4 = (f32[1,1,64]{2,1,0:T(1,128)S(1)}, f32[1,1,64]{2,1,0:T(1,128)}, u32[]{:S(2)}) copy-start(f32[1,1,64]{2,1,0:T(1,128)} %param.14) | copy-start | bytes 772
  1.4 1.2 %copy-start = (bf16[1,1,4,1024,128]{4,3,2,1,0:T(8,128)(2,1)S(1)}, bf16[1,1,4,1024,128]{4,3,2,1,0:T(8,128)(2,1)}, u32[]{:S(2)}) copy-start(bf16[1,1,4,1024,128]{4,3,2,1,0:T(8,128)(2,1)} %param.11) | copy-start | bytes 3145732
  2.6 0.9 %copy-start.1 = (bf16[1,1,80,1024]{3,2,1,0:T(8,128)(2,1)S(1)}, bf16[1,1,80,1024]{3,2,1,0:T(8,128)(2,1)}, u32[]{:S(2)}) copy-start(bf16[1,1,80,1024]{3,2,1,0:T(8,128)(2,1)} %param.10) | copy-start | bytes 491524
  3.5 20.9 %copy-start.8 = (f32[1,1,80,12,128]{4,2,3,1,0:T(8,128)S(1)}, f32[1,1,80,12,128]{4,2,3,1,0:T(8,128)}, u32[]{:S(2)}) copy-start(f32[1,1,80,12,128]{4,2,3,1,0:T(8,128)} %param.9) | copy-start | bytes 1474564

commit v2 on v1

v2 whole, which is shorter than its diff:
```python
import functools

import jax
import jax.numpy as jnp
from jax import lax
from jax.experimental import pallas as pl
from jax.experimental.pallas import tpu as pltpu
from jax.sharding import PartitionSpec as P

MEM = 80
AX = 8
AY = 16
OCN_DEV = 1024
OB = 32
NB = 2
K = 4
FIELDS = 12
COMP = 13
CELLS = 128
OBS = 64
ROWS = 88
GROUPS = 11
CHUNKS = 4
CW = OCN_DEV // CHUNKS
DIRECT = 3

MESH = pl.DeviceIdType.MESH
NEAR = [(dx, dy) for dx in (-1, 0, 1) for dy in (-1, 0, 1)]
AROUND = [d for d in NEAR if d != (0, 0)]


def slot(dx, dy):
    return (dx + 1) * 3 + dy + 1


def roll(x, shift):
    shift = shift % CELLS
    return x if shift == 0 else pltpu.roll(x, shift, 1)


def exchange_kernel(
    src_hbm,
    ocean,
    weights,
    cell_hbm,
    value_hbm,
    error_hbm,
    live_hbm,
    order_hbm,
    f_out,
    obs_out,
    src,
    ints,
    floats,
    oce,
    wv,
    acc,
    columns,
    meta,
    meta_in,
    pack_y,
    pack_x,
    in_w,
    in_e,
    in_n,
    in_s,
    local_sem,
    oce_send,
    oce_recv,
    relay_send,
    meta_send,
    meta_recv,
    halo_send,
    halo_recv,
):
    i = lax.axis_index("gx")
    j = lax.axis_index("gy")
    nx = lax.axis_size("gx")
    ny = lax.axis_size("gy")

    away = 2 * (i % 2) - 1
    mate = -away
    has_away = jnp.logical_and(i + away >= 0, i + away < nx)
    near = 1 - 2 * ((j % 4 + 3) // 4)
    far = -near
    has_far = jnp.logical_and(j + far >= 0, j + far < ny)
    when_away, when_far = pl.when(has_away), pl.when(has_far)

    def has(dx, dy):
        cond = None
        for pos, step, count in ((i, dx, nx), (j, dy, ny)):
            if step:
                ok = (pos > 0) if step < 0 else (pos < count - 1)
                cond = ok if cond is None else jnp.logical_and(cond, ok)
        return cond

    def when(dx, dy):
        return pl.when(has(dx, dy))

    def device(dx, dy):
        return (i + dx, j + dy)

    barrier = pltpu.get_barrier_semaphore()

    def greet(dx, dy):
        pl.semaphore_signal(barrier, inc=1, device_id=device(dx, dy), device_id_type=MESH)

    @when_far
    def _():
        greet(0, far)

    greet(0, near)

    @when_away
    def _():
        greet(away, 0)

    greet(mate, 0)

    own_load = [
        pltpu.make_async_copy(
            ocean.at[:, pl.ds(c * CW, CW)], oce.at[4, c], local_sem.at[c]
        )
        for c in range(CHUNKS)
    ]
    for copy in own_load:
        copy.start()
    small_load = [
        pltpu.make_async_copy(source, target, local_sem.at[CHUNKS + 1 + n])
        for n, (source, target) in enumerate(
            (
                (cell_hbm, ints.at[0]),
                (live_hbm, ints.at[1]),
                (order_hbm, ints.at[2]),
                (value_hbm, floats.at[0]),
                (error_hbm, floats.at[1]),
                (src_hbm, src),
            )
        )
    ]
    for copy in small_load:
        copy.start()
    w_load = pltpu.make_async_copy(weights, wv, local_sem.at[CHUNKS])
    w_load.start()

    pl.semaphore_wait(
        barrier,
        2 + has_away.astype(jnp.int32) + has_far.astype(jnp.int32),
    )

    def ocean_copy(c, dx, dy, sem):
        return pltpu.make_async_remote_copy(
            src_ref=oce.at[4, c],
            dst_ref=oce.at[slot(-dx, -dy), c],
            send_sem=oce_send.at[sem, c],
            recv_sem=oce_recv.at[slot(-dx, -dy), c],
            device_id=device(dx, dy),
            device_id_type=MESH,
        )

    def relay_copy(c, dx, dy, sem):
        return pltpu.make_async_remote_copy(
            src_ref=oce.at[slot(0, dy), c],
            dst_ref=oce.at[slot(-dx, dy), c],
            send_sem=relay_send.at[sem, c],
            recv_sem=oce_recv.at[slot(-dx, dy), c],
            device_id=device(dx, 0),
            device_id_type=MESH,
        )

    def arrived(c, dx, dy):
        ocean_copy(c, -dx, -dy, 0).wait_recv()

    def meta_copy(dx, dy):
        return pltpu.make_async_remote_copy(
            src_ref=meta,
            dst_ref=meta_in.at[slot(-dx, -dy)],
            send_sem=meta_send.at[slot(dx, dy)],
            recv_sem=meta_recv.at[slot(-dx, -dy)],
            device_id=device(dx, dy),
            device_id_type=MESH,
        )

    for c in range(CHUNKS):
        own_load[c].wait()

        @when_far
        def _():
            ocean_copy(c, 0, far, 1).start()

        ocean_copy(c, 0, near, 0).start()

        @when_away
        def _():
            ocean_copy(c, away, 0, 3).start()

        ocean_copy(c, mate, 0, 2).start()

    for copy in small_load:
        copy.wait()
    lane = lax.broadcasted_iota(jnp.int32, (OBS, OBS), 0)
    perm = jnp.where(lane == ints[2], 1.0, 0.0)
    rows = [
        ints[0].astype(jnp.float32),
        floats[0],
        floats[1],
        ints[1].astype(jnp.float32),
    ]
    stacked = jnp.concatenate(rows + [jnp.zeros((4, OBS), jnp.float32)], axis=0)
    ordered = jnp.dot(
        stacked,
        perm,
        precision=lax.Precision.HIGHEST,
        preferred_element_type=jnp.float32,
    )
    meta[...] = jnp.concatenate([ordered, jnp.zeros((8, CELLS - OBS), jnp.float32)], axis=1)

    positions = [
        (src[0, k] // ny - i + 1) * 3 + (src[0, k] % ny - j + 1) for k in range(K)
    ]

    def product(dx, dy, c):
        p = slot(dx, dy)
        which = jnp.int32(0)
        valid = positions[0] == p
        for k in range(1, K):
            which = jnp.where(positions[k] == p, k, which)
            valid = jnp.logical_or(valid, positions[k] == p)
        part = jnp.dot(
            oce[p, c],
            wv[which, pl.ds(c * CW, CW), :],
            preferred_element_type=jnp.float32,
        )
        return jnp.where(valid, part, 0.0)

    w_load.wait()
    total = product(0, 0, 0)
    for c in range(1, CHUNKS):
        total = total + product(0, 0, c)
    acc[...] = total

    def pass_on(c, dy, index):
        relay_copy(c, mate, dy, 2 * index).start()

        @when_away
        def _():
            if c < DIRECT:
                relay_copy(c, away, dy, 2 * index + 1).start()
            if c == 0:
                for direct in range(DIRECT, CHUNKS):
                    ocean_copy(direct, away, dy, 4 + index).start()

    for step in range(CHUNKS + 1):
        if step < CHUNKS:
            arrived(step, 0, near)
            pass_on(step, near, 0)
        if step > 0:

            @when_far
            def _():
                arrived(step - 1, 0, far)
                pass_on(step - 1, far, 1)

        if step == 1:
            for dx, dy in AROUND:

                @when(dx, dy)
                def _():
                    meta_copy(dx, dy).start()

        if step < CHUNKS:
            arrived(step, mate, 0)
            acc[...] += product(mate, 0, step) + product(0, near, step)

            @when_away
            def _():
                arrived(step, away, 0)
                acc[...] += product(away, 0, step)

        if step > 0:

            @when_far
            def _():
                acc[...] += product(0, far, step - 1)

    for c in range(CHUNKS):
        arrived(c, mate, near)
        acc[...] += product(mate, near, c)

        @when_far
        def _():
            arrived(c, mate, far)
            acc[...] += product(mate, far, c)

    for c in range(CHUNKS):

        @when_away
        def _():
            arrived(c, away, near)
            acc[...] += product(away, near, c)

            @when_far
            def _():
                arrived(c, away, far)
                acc[...] += product(away, far, c)

    sst = acc[...]
    mean = jnp.sum(sst, axis=0, keepdims=True) / MEM
    anomaly = sst - mean
    pieces = [anomaly[8 * g : 8 * g + 8] for g in range(MEM // 8)]
    pieces.append(jnp.broadcast_to(mean, (8, CELLS)))
    lane8 = lax.broadcasted_iota(jnp.int32, (8, CELLS), 1)
    pair = (lane8 % AY) // 2
    quarter = lane8 // 32

    for block in range(2):
        west = jnp.zeros((8, CELLS), jnp.float32)
        east = west
        for g in range(8 * block, min(8 * block + 8, GROUPS)):
            s = g % 8
            west = jnp.where(pair == s, roll(pieces[g], 2 * s), west)
            east = jnp.where(pair == 7 - s, roll(pieces[g], -2 * s), east)
        pack_y[0, 8 * block : 8 * block + 8, :] = west
        pack_y[1, 8 * block : 8 * block + 8, :] = east
    for block in range(3):
        north = jnp.zeros((8, CELLS), jnp.float32)
        south = north
        for g in range(4 * block, min(4 * block + 4, GROUPS)):
            s = g % 4
            north = jnp.where(quarter == s, roll(pieces[g], 32 * s), north)
            south = jnp.where(quarter == 3 - s, roll(pieces[g], -32 * s), south)
        pack_x[0, 8 * block : 8 * block + 8, :] = north
        pack_x[1, 8 * block : 8 * block + 8, :] = south

    def halo_copy(dx, dy):
        if dy < 0:
            source, target = pack_y.at[0], in_w.at[1 - dx]
        elif dy > 0:
            source, target = pack_y.at[1], in_e.at[1 - dx]
        elif dx < 0:
            source, target = pack_x.at[0], in_n
        else:
            source, target = pack_x.at[1], in_s
        return pltpu.make_async_remote_copy(
            src_ref=source,
            dst_ref=target,
            send_sem=halo_send.at[slot(dx, dy)],
            recv_sem=halo_recv.at[slot(-dx, -dy)],
            device_id=device(dx, dy),
            device_id_type=MESH,
        )

    f_out[0, :MEM, :] = anomaly
    f_out[0, MEM:, :] = pieces[-1]

    for dx, dy in ((1, 1), (1, -1), (-1, 1), (-1, -1), (0, 1), (0, -1), (1, 0), (-1, 0)):

        @when(dx, dy)
        def _():
            halo_copy(dx, dy).start()

    absent = jnp.where(lax.broadcasted_iota(jnp.int32, (8, CELLS), 0) == 2, 1.0, 0.0)
    for dx, dy in AROUND:

        @when(dx, dy)
        def _():
            meta_copy(-dx, -dy).wait_recv()

    blocks = []
    for dx, dy in NEAR:
        if (dx, dy) == (0, 0):
            blocks.append(meta[...])
        else:
            blocks.append(jnp.where(has(dx, dy), meta_in[slot(dx, dy)], absent))
    blocks.append(jnp.zeros((CELLS - 72, CELLS), jnp.float32))
    columns[...] = jnp.concatenate(blocks, axis=0).T

    lane32 = lax.broadcasted_iota(jnp.int32, (OB, CELLS), 1)
    lanes = lane32.astype(jnp.float32)
    low_x32, low_y32 = lane32 < 64, (lane32 % AY) < 8
    for batch in range(NB):
        rows = slice(batch * OB, (batch + 1) * OB)

        def dense(dx, dy):
            at = 8 * slot(dx, dy)
            cells, values, errors, alive = (
                jnp.broadcast_to(columns[rows, at + n : at + n + 1], (OB, CELLS))
                for n in range(4)
            )
            hit = jnp.where(cells == lanes, alive, 0.0)
            return hit, hit * values, errors + (1.0 - alive), errors

        def either(mask, first, second):
            return tuple(jnp.where(mask, a, b) for a, b in zip(first, second))

        places = [
            lambda: dense(0, 0),
            lambda: either(low_x32, dense(1, 0), dense(-1, 0)),
            lambda: either(low_y32, dense(0, 1), dense(0, -1)),
            lambda: either(
                low_y32,
                either(low_x32, dense(1, 1), dense(-1, 1)),
                either(low_x32, dense(1, -1), dense(-1, -1)),
            ),
        ]
        for f, place in enumerate(places):
            for n, part in enumerate(place()):
                obs_out[batch, f, n] = part

    for c in range(CHUNKS):
        ocean_copy(c, 0, near, 0).wait_send()
        ocean_copy(c, mate, 0, 2).wait_send()
        relay_copy(c, mate, near, 0).wait_send()

        @when_far
        def _():
            ocean_copy(c, 0, far, 1).wait_send()
            relay_copy(c, mate, far, 2).wait_send()

        @when_away
        def _():
            ocean_copy(c, away, 0, 3).wait_send()
            for dy, index, there in ((near, 0, None), (far, 1, has_far)):

                def finish():
                    if c < DIRECT:
                        relay_copy(c, away, dy, 2 * index + 1).wait_send()
                    else:
                        ocean_copy(c, away, dy, 4 + index).wait_send()

                finish() if there is None else pl.when(there)(finish)

    for dx, dy in AROUND:

        @when(dx, dy)
        def _():
            meta_copy(dx, dy).wait_send()

    for dx, dy in AROUND:

        @when(dx, dy)
        def _():
            halo_copy(-dx, -dy).wait_recv()

    low_y = (lane8 % AY) < 8
    low_x = lane8 < 64
    zero = jnp.zeros((8, CELLS), jnp.float32)

    def present(ref, dx, dy):
        return jnp.where(has(dx, dy), ref[...], 0.0)

    north = present(in_n, 1, 0)
    south = present(in_s, -1, 0)
    west = present(in_w.at[1], 0, 1)
    east = present(in_e.at[1], 0, -1)
    low16 = lax.broadcasted_iota(jnp.int32, (16, CELLS), 1) < 64
    west_c = jnp.where(low16, present(in_w.at[2], 1, 1), present(in_w.at[0], -1, 1))
    east_c = jnp.where(low16, present(in_e.at[2], 1, -1), present(in_e.at[0], -1, -1))
    for g in range(GROUPS):
        at = pl.ds(8 * g, 8)
        b, s = g // 4, g % 4
        f_out[1, at, :] = jnp.where(
            low_x,
            roll(north[8 * b : 8 * b + 8], -32 * s),
            roll(south[8 * b : 8 * b + 8], 32 * s),
        )
        b, s = g // 8, g % 8
        for place, w, e in ((2, west, east), (3, west_c, east_c)):
            f_out[place, at, :] = jnp.where(
                low_y,
                roll(w[8 * b : 8 * b + 8], -2 * s),
                roll(e[8 * b : 8 * b + 8], 2 * s),
            )

    for dx, dy in AROUND:

        @when(dx, dy)
        def _():
            halo_copy(dx, dy).wait_send()


def update_kernel(
    f_in,
    obs,
    atm,
    mean_out,
    anom_out,
    state,
    shifted,
    factors,
    result,
    means,
    out_sem,
    mean_sem,
):
    lane8 = lax.broadcasted_iota(jnp.int32, (8, CELLS), 1)
    y8 = lane8 % AY
    first_y, last_y = y8 == 0, y8 == AY - 1
    first_x, last_x = lane8 < AY, lane8 >= CELLS - AY
    groups = range(MEM // 8)

    def at(g):
        return slice(8 * g, 8 * g + 8)

    def shift_all(blocks, wanted):
        out = {}
        turned = {}
        for f in range(4):
            if any((f ^ a) in wanted for a in (0, 1)):
                other = blocks[f ^ 2]
                turned[f, 0] = blocks[f]
                turned[f, 1] = jnp.where(last_y, roll(other, 15), roll(blocks[f], -1))
                turned[f, -1] = jnp.where(first_y, roll(other, -15), roll(blocks[f], 1))
        for f in wanted:
            for dy in (-1, 0, 1):
                own, other = turned[f, dy], turned[f ^ 1, dy]
                out[f, slot(0, dy)] = own
                out[f, slot(1, dy)] = roll(jnp.where(first_x, other, own), -AY)
                out[f, slot(-1, dy)] = roll(jnp.where(last_x, other, own), AY)
        return out

    def allsum(x):
        for step in (4, 2, 1):
            x = x + pltpu.roll(x, step, 0)
        return x

    zero = jnp.zeros((8, CELLS), jnp.float32)
    tapers = [
        max(1.0 - (dx * dx + dy * dy) / 4.0, 0.0) ** 2 / (MEM - 1) for dx, dy in NEAR
    ]

    for batch in range(NB):
        source = f_in if batch == 0 else state
        wanted = (0, 1, 2, 3) if batch == 0 else (0,)
        base = 0 if batch == 0 else 36

        alphas, betas = [], []
        for f in range(4):
            square = zero
            for g in groups:
                block = source[f, at(g), :]
                square = square + block * block
            variance = allsum(square) / (MEM - 1)
            total = [zero, zero, zero]
            for q in range(OB // 8):
                masked = obs[batch, f, 0, at(q), :]
                masked_value = obs[batch, f, 1, at(q), :]
                inverse = 1.0 / (variance + obs[batch, f, 2, at(q), :])
                ratio = obs[batch, f, 3, at(q), :] * inverse
                damping = 1.0 / (1.0 + ratio * lax.rsqrt(ratio))
                weighting = masked * inverse
                total[0] = total[0] + weighting * damping
                total[1] = total[1] + weighting
                total[2] = total[2] + masked_value * inverse
            betas.append(allsum(total[0]))
            alphas.append(allsum(total[2]) - source[f, MEM:, :] * allsum(total[1]))
        alphas = shift_all(alphas, wanted)
        betas = shift_all(betas, wanted)
        alphas = {key: alphas[key] * tapers[key[1]] for key in alphas}
        betas = {key: betas[key] * tapers[key[1]] for key in betas}
        for d in range(9):
            factors[batch, 0, d] = alphas[0, d]
            factors[batch, 1, d] = betas[0, d]

        for g in groups:
            moved = shift_all([source[f, at(g), :] for f in range(4)], wanted)
            for f in wanted:
                for d in range(9):
                    shifted[base + 9 * f + d, at(g), :] = moved[f, d]

        for f in wanted:
            sums = [zero] * 9
            for g in groups:
                block = source[f, at(g), :]
                for d in range(9):
                    sums[d] = sums[d] + shifted[base + 9 * f + d, at(g), :] * block
            sums = [allsum(x) for x in sums]
            mean = source[f, MEM:, :]
            for d in range(9):
                mean = mean + alphas[f, d] * sums[d]
            gains = [betas[f, d] * sums[d] for d in range(9)]
            for g in groups:
                block = source[f, at(g), :]
                for d in range(9):
                    block = block - shifted[base + 9 * f + d, at(g), :] * gains[d]
                if batch + 1 < NB:
                    state[f, at(g), :] = block
                else:
                    result[FIELDS, at(g), :] = block
            if batch + 1 < NB:
                state[f, MEM:, :] = mean
            else:
                means[FIELDS] = mean[:1]

    def sst_copy():
        return pltpu.make_async_copy(result.at[FIELDS], anom_out.at[FIELDS], mean_sem.at[1])

    def field_copy(pair):
        part = pl.ds(2 * pair, 2)
        return pltpu.make_async_copy(result.at[part], anom_out.at[part], out_sem.at[pair])

    sst_copy().start()

    def two_fields(pair, carry):
        fields = (2 * pair, 2 * pair + 1)
        sums = [zero, zero]
        for g in groups:
            for u in range(2):
                sums[u] = sums[u] + atm[fields[u], at(g), :]
        mean = [allsum(x) / MEM for x in sums]
        for batch in range(NB):
            sums = [[zero] * 9, [zero] * 9]
            for g in groups:
                for u in range(2):
                    if batch == 0:
                        block = atm[fields[u], at(g), :] - mean[u]
                        result[fields[u], at(g), :] = block
                    else:
                        block = result[fields[u], at(g), :]
                    for d in range(9):
                        sums[u][d] = sums[u][d] + shifted[36 * batch + d, at(g), :] * block
            sums = [[allsum(x) for x in sums[u]] for u in range(2)]
            for u in range(2):
                for d in range(9):
                    mean[u] = mean[u] + factors[batch, 0, d] * sums[u][d]
            gains = [[factors[batch, 1, d] * sums[u][d] for d in range(9)] for u in range(2)]
            for g in groups:
                for u in range(2):
                    block = result[fields[u], at(g), :]
                    for d in range(9):
                        block = block - shifted[36 * batch + d, at(g), :] * gains[u][d]
                    result[fields[u], at(g), :] = block
        for u in range(2):
            means[fields[u]] = mean[u][:1]
        field_copy(pair).start()
        return carry

    lax.fori_loop(0, FIELDS // 2, two_fields, 0)
    mean_copy = pltpu.make_async_copy(means, mean_out, mean_sem.at[0])
    mean_copy.start()
    sst_copy().wait()
    for pair in range(FIELDS // 2):
        field_copy(pair).wait()
    mean_copy.wait()


def local(
    atm_members,
    ocean_members,
    remap_weights,
    pair_src,
    obs_cell,
    obs_value,
    obs_error,
    obs_live,
    obs_order,
):
    f32 = jnp.float32
    vmem = pl.BlockSpec(memory_space=pltpu.VMEM)
    hbm = pl.BlockSpec(memory_space=pltpu.HBM)
    dma = pltpu.SemaphoreType.DMA
    state, meta = pl.pallas_call(
        exchange_kernel,
        out_shape=(
            jax.ShapeDtypeStruct((4, ROWS, CELLS), f32),
            jax.ShapeDtypeStruct((NB, 4, 4, OB, CELLS), f32),
        ),
        in_specs=[hbm] * 8,
        out_specs=(vmem, vmem),
        scratch_shapes=[
            pltpu.SMEM((1, K), jnp.int32),
            pltpu.VMEM((3, 1, OBS), jnp.int32),
            pltpu.VMEM((2, 1, OBS), f32),
            pltpu.VMEM((9, CHUNKS, MEM, CW), jnp.bfloat16),
            pltpu.VMEM((K, OCN_DEV, CELLS), jnp.bfloat16),
            pltpu.VMEM((MEM, CELLS), f32),
            pltpu.VMEM((CELLS, CELLS), f32),
            pltpu.VMEM((8, CELLS), f32),
            pltpu.VMEM((9, 8, CELLS), f32),
            pltpu.VMEM((2, 16, CELLS), f32),
            pltpu.VMEM((2, 24, CELLS), f32),
            pltpu.VMEM((3, 16, CELLS), f32),
            pltpu.VMEM((3, 16, CELLS), f32),
            pltpu.VMEM((24, CELLS), f32),
            pltpu.VMEM((24, CELLS), f32),
            dma((CHUNKS + 7,)),
            dma((9, CHUNKS)),
            dma((9, CHUNKS)),
            dma((9, CHUNKS)),
            dma((9,)),
            dma((9,)),
            dma((9,)),
            dma((9,)),
        ],
        compiler_params=pltpu.CompilerParams(
            collective_id=0, has_side_effects=True, vmem_limit_bytes=16 * 1024 * 1024
        ),
    )(
        *(
            pltpu.with_memory_space_constraint(x, pltpu.HBM)
            for x in (
                pair_src[0],
                ocean_members[0, 0],
                remap_weights[0, 0],
                obs_cell[0],
                obs_value[0],
                obs_error[0],
                obs_live[0],
                obs_order[0],
            )
        )
    )
    mean, anomaly = pl.pallas_call(
        update_kernel,
        out_shape=(
            jax.ShapeDtypeStruct((COMP, 1, CELLS), f32),
            jax.ShapeDtypeStruct((COMP, MEM, CELLS), f32),
        ),
        in_specs=[vmem] * 3,
        out_specs=(hbm, hbm),
        scratch_shapes=[
            pltpu.VMEM((4, ROWS, CELLS), f32),
            pltpu.VMEM((45, MEM, CELLS), f32),
            pltpu.VMEM((NB, 2, 9, 8, CELLS), f32),
            pltpu.VMEM((COMP, MEM, CELLS), f32),
            pltpu.VMEM((COMP, 1, CELLS), f32),
            dma((FIELDS // 2,)),
            dma((2,)),
        ],
        compiler_params=pltpu.CompilerParams(vmem_limit_bytes=16 * 1024 * 1024),
    )(state, meta, jnp.transpose(atm_members[0, 0], (1, 0, 2)))
    return (mean.reshape(1, 1, COMP, CELLS), jnp.transpose(anomaly, (1, 0, 2))[None, None])


def solution(mesh):
    in_specs = (
        P("gx", "gy", None, None, None),
        P("gx", "gy", None, None),
        P("gx", "gy", None, None, None),
        P("gx", "gy", None),
        P("gx", "gy", None),
        P("gx", "gy", None),
        P("gx", "gy", None),
        P("gx", "gy", None),
        P("gx", "gy", None),
    )
    out_specs = (P("gx", "gy", None, None), P("gx", "gy", None, None, None))
    return jax.shard_map(local, mesh=mesh, in_specs=in_specs, out_specs=out_specs, check_vma=False)
```

time: 31.1 us -> 24.3 us (0.78)
  local copies, waits for them, and re-layouts: 4.56 us -> 0.01 us
  Pallas kernels: 25.7 us -> 23.5 us
    unnamed x21 -> x2, local copies, waits for them, and re-layouts: 4.56 us -> 0.01 us
    pallas_call x1, Pallas kernels: 20.9 us -> 19.2 us  [local(): pl.pallas_call(exchange_kernel, out_shape=(jax.ShapeDtypeStruct((4, ROWS,...]
    pallas_call x1, Pallas kernels: 4.75 us -> 4.35 us  [local(): pl.pallas_call(update_kernel, out_shape=(jax.ShapeDtypeStruct((COMP, 1, C...]
where the time goes in v2:
time: 24.3 us; the launch traced here: 24.2 us
  Pallas kernels  23.5 us (97%)
  between operations  0.66 us (3%)
    pallas_call x1, Pallas kernels, local(): pl.pallas_call(exchange_kernel, out_shape=(jax.ShapeDtypeStruct((4, ROWS,...  19.2 us
    pallas_call x1, Pallas kernels, local(): pl.pallas_call(update_kernel, out_shape=(jax.ShapeDtypeStruct((COMP, 1, C...  4.35 us

profile of v2, /device:TPU:7, one launch (start us, length us, event | category | flops | bytes accessed | tf_op | source)
XLA Modules:
  0.0 24.2 jit_solution(2014674887198675338)
XLA Ops:
  0.6 0.0 copy-start
  0.6 19.2 %shard_map.104 = (f32[4,88,128]{2,1,0:T(8,128)S(1)}, f32[2,4,4,32,128]{4,3,2,1,0:T(8,128)S(1)}) custom-call(s32[1,4]{1,0:T(1,128)} %bitcast.20, bf16[80,1024]{1,0:T(8,128)(2,1)} %bitcast.19, bf16[4,1024,128]{2,1,0:T(8,128)(2,1)} %bitcast.18, s32[1,64]{1,0:T(1,128)} %bitcast.21, f32[1,64]{1,0:T(1,128)} %bitcast.22, f32[1,64]{1,0:T(1,128)} %bitcast.23, ...), custom_call_target="tpu_custom_call" | custom-call | tf_op jit(solution)/shard_map/pallas_call | solution.py:662
  19.8 0.0 copy-done
  19.8 4.3 %shard_map.105 = (f32[13,1,128]{2,1,0:T(1,128)}, f32[13,80,128]{2,1,0:T(8,128)}) custom-call(f32[4,88,128]{2,1,0:T(8,128)S(1)} %get-tuple-element.6.f_in, f32[2,4,4,32,128]{4,3,2,1,0:T(8,128)S(1)} %get-tuple-element.7.obs, f32[12,80,128]{2,1,0:T(8,128)S(1)} %bitcast.17), custom_call_target="tpu_custom_call" | custom-call | tf_op jit(solution)/shard_map/pallas_call | solution.py:713
Async XLA Ops:
  0.6 19.2 %copy-start = (f32[1,1,80,12,128]{4,2,3,1,0:T(8,128)S(1)}, f32[1,1,80,12,128]{4,2,3,1,0:T(8,128)}, u32[]{:S(2)}) copy-start(f32[1,1,80,12,128]{4,2,3,1,0:T(8,128)} %param.9) | copy-start | bytes 1474564

commit v3 on v2

--- a/solution.py
+++ b/solution.py
@@ -22,7 +22,7 @@
 GROUPS = 11
 CHUNKS = 4
 CW = OCN_DEV // CHUNKS
-DIRECT = 3
+FIRST, SECOND, THIRD, BOTH, WHOLE = (0, 1), (1, 1), (2, 2), (0, 2), (0, 4)
 
 MESH = pl.DeviceIdType.MESH
 NEAR = [(dx, dy) for dx in (-1, 0, 1) for dy in (-1, 0, 1)]
@@ -56,18 +56,14 @@
     wv,
     acc,
     columns,
-    meta,
     meta_in,
     pack_y,
     pack_x,
-    in_w,
-    in_e,
-    in_n,
-    in_s,
+    in_y,
+    in_x,
     local_sem,
     oce_send,
     oce_recv,
-    relay_send,
     meta_send,
     meta_recv,
     halo_send,
@@ -100,23 +96,6 @@
     def device(dx, dy):
         return (i + dx, j + dy)
 
-    barrier = pltpu.get_barrier_semaphore()
-
-    def greet(dx, dy):
-        pl.semaphore_signal(barrier, inc=1, device_id=device(dx, dy), device_id_type=MESH)
-
-    @when_far
-    def _():
-        greet(0, far)
-
-    greet(0, near)
-
-    @when_away
-    def _():
-        greet(away, 0)
-
-    greet(mate, 0)
-
     own_load = [
         pltpu.make_async_copy(
             ocean.at[:, pl.ds(c * CW, CW)], oce.at[4, c], local_sem.at[c]
@@ -125,6 +104,87 @@
     ]
     for copy in own_load:
         copy.start()
+
+    barrier = pltpu.get_barrier_semaphore()
+
+    def greet(dx, dy):
+        pl.semaphore_signal(barrier, inc=1, device_id=device(dx, dy), device_id_type=MESH)
+
+    @when_far
+    def _():
+        greet(0, far)
+
+    greet(0, near)
+
+    @when_away
+    def _():
+        greet(away, 0)
+
+    greet(mate, 0)
+
+    pl.semaphore_wait(
+        barrier,
+        2 + has_away.astype(jnp.int32) + has_far.astype(jnp.int32),
+    )
+
+    def tile(p, piece):
+        return oce.at[p, pl.ds(*piece)]
+
+    def ocean_copy(piece, from_dx, from_dy, dx, dy, sem):
+        target = slot(from_dx - dx, from_dy - dy)
+        return pltpu.make_async_remote_copy(
+            src_ref=tile(slot(from_dx, from_dy), piece),
+            dst_ref=tile(target, piece),
+            send_sem=oce_send.at[sem],
+            recv_sem=oce_recv.at[target, piece[0]],
+            device_id=device(dx, dy),
+            device_id_type=MESH,
+        )
+
+    def arrived(piece, dx, dy):
+        ocean_copy(piece, 0, 0, -dx, -dy, 0).wait_recv()
+
+    def meta_copy(dx, dy, sem):
+        if isinstance(dx, int):
+            source, target = meta_in.at[4], meta_in.at[slot(0, -dy)]
+            recv = meta_recv.at[slot(0, -dy)]
+        else:
+            source, target = meta_in.at[pl.ds(3, 3)], meta_in.at[pl.ds(slot(-dx, -1), 3)]
+            recv = meta_recv.at[slot(-dx, 0)]
+        return pltpu.make_async_remote_copy(
+            src_ref=source,
+            dst_ref=target,
+            send_sem=meta_send.at[sem],
+            recv_sem=recv,
+            device_id=device(dx, dy),
+            device_id_type=MESH,
+        )
+
+    sends = []
+
+    def send(far_needed, away_needed, *spec):
+        sends.append((far_needed, away_needed, spec + (len(sends),)))
+        ocean_copy(*sends[-1][2]).start()
+
+    for c in range(CHUNKS):
+        own_load[c].wait()
+        if c == 0:
+            send(False, False, FIRST, 0, 0, 0, near)
+            when_far(lambda: send(True, False, FIRST, 0, 0, 0, far))
+        if c == 1:
+            send(False, False, SECOND, 0, 0, 0, near)
+            when_far(lambda: send(True, False, SECOND, 0, 0, 0, far))
+        if c == 3:
+
+            @when_away
+            def _():
+                send(False, True, THIRD, 0, 0, away, 0)
+                send(False, True, BOTH, 0, 0, away, 0)
+
+            send(False, False, THIRD, 0, 0, 0, near)
+            when_far(lambda: send(True, False, THIRD, 0, 0, 0, far))
+            send(False, False, WHOLE, 0, 0, mate, 0)
+
     small_load = [
         pltpu.make_async_copy(source, target, local_sem.at[CHUNKS + 1 + n])
         for n, (source, target) in enumerate(
@@ -142,59 +202,6 @@
         copy.start()
     w_load = pltpu.make_async_copy(weights, wv, local_sem.at[CHUNKS])
     w_load.start()
-
-    pl.semaphore_wait(
-        barrier,
-        2 + has_away.astype(jnp.int32) + has_far.astype(jnp.int32),
-    )
-
-    def ocean_copy(c, dx, dy, sem):
-        return pltpu.make_async_remote_copy(
-            src_ref=oce.at[4, c],
-            dst_ref=oce.at[slot(-dx, -dy), c],
-            send_sem=oce_send.at[sem, c],
-            recv_sem=oce_recv.at[slot(-dx, -dy), c],
-            device_id=device(dx, dy),
-            device_id_type=MESH,
-        )
-
-    def relay_copy(c, dx, dy, sem):
-        return pltpu.make_async_remote_copy(
-            src_ref=oce.at[slot(0, dy), c],
-            dst_ref=oce.at[slot(-dx, dy), c],
-            send_sem=relay_send.at[sem, c],
-            recv_sem=oce_recv.at[slot(-dx, dy), c],
-            device_id=device(dx, 0),
-            device_id_type=MESH,
-        )
-
-    def arrived(c, dx, dy):
-        ocean_copy(c, -dx, -dy, 0).wait_recv()
-
-    def meta_copy(dx, dy):
-        return pltpu.make_async_remote_copy(
-            src_ref=meta,
-            dst_ref=meta_in.at[slot(-dx, -dy)],
-            send_sem=meta_send.at[slot(dx, dy)],
-            recv_sem=meta_recv.at[slot(-dx, -dy)],
-            device_id=device(dx, dy),
-            device_id_type=MESH,
-        )
-
-    for c in range(CHUNKS):
-        own_load[c].wait()
-
-        @when_far
-        def _():
-            ocean_copy(c, 0, far, 1).start()
-
-        ocean_copy(c, 0, near, 0).start()
-
-        @when_away
-        def _():
-            ocean_copy(c, away, 0, 3).start()
-
-        ocean_copy(c, mate, 0, 2).start()
 
     for copy in small_load:
         copy.wait()
@@ -213,7 +220,12 @@
         precision=lax.Precision.HIGHEST,
         preferred_element_type=jnp.float32,
     )
-    meta[...] = jnp.concatenate([ordered, jnp.zeros((8, CELLS - OBS), jnp.float32)], axis=1)
+    meta_in[4] = jnp.concatenate([ordered, jnp.zeros((8, CELLS - OBS), jnp.float32)], axis=1)
+
+    @pl.when(jnp.logical_not(has_far))
+    def _():
+        meta_in[slot(0, far)] = jnp.zeros((8, CELLS), jnp.float32)
+
 
     positions = [
         (src[0, k] // ny - i + 1) * 3 + (src[0, k] % ny - j + 1) for k in range(K)
@@ -239,70 +251,64 @@
         total = total + product(0, 0, c)
     acc[...] = total
 
-    def pass_on(c, dy, index):
-        relay_copy(c, mate, dy, 2 * index).start()
+    def add(dx, dy, piece):
+        for c in range(piece[0], piece[0] + piece[1]):
+            acc[...] += product(dx, dy, c)
+
+    def from_y(piece, with_away):
+        def one(dy, is_far):
+            arrived(piece, 0, dy)
+            send(is_far, False, piece, 0, dy, mate, 0)
+            if with_away:
+                when_away(lambda: send(is_far, True, piece, 0, dy, away, 0))
+
+        one(near, False)
+        when_far(lambda: one(far, True))
+
+    from_y(FIRST, True)
+    meta_copy(0, near, 0).start()
+    when_far(lambda: meta_copy(0, far, 1).start())
+
+    @when_away
+    def _():
+        arrived(THIRD, away, 0)
+        send(False, True, THIRD, away, 0, 0, near)
+        when_far(lambda: send(True, True, THIRD, away, 0, 0, far))
+
+    from_y(SECOND, True)
+    arrived(WHOLE, mate, 0)
+    add(mate, 0, WHOLE)
+    add(0, near, BOTH)
+    when_far(lambda: add(0, far, BOTH))
+    when_away(lambda: add(away, 0, THIRD))
+    from_y(THIRD, False)
+    add(0, near, THIRD)
+    when_far(lambda: add(0, far, THIRD))
+
+    meta_copy(0, -near, 0).wait_recv()
+    when_far(lambda: meta_copy(0, -far, 1).wait_recv())
+    meta_copy(mate, 0, 2).start()
+    when_away(lambda: meta_copy(away, 0, 3).start())
+
+    @when_away
+    def _():
+        arrived(BOTH, away, 0)
+        add(away, 0, BOTH)
+
+    def corner(dx, dy, piece):
+        arrived(piece, dx, dy)
+        add(dx, dy, piece)
+
+    for piece in (FIRST, SECOND, THIRD):
+        corner(mate, near, piece)
+        when_far(lambda: corner(mate, far, piece))
+
+    for piece in (FIRST, SECOND, THIRD):
 
         @when_away
         def _():
-            if c < DIRECT:
-                relay_copy(c, away, dy, 2 * index + 1).start()
-            if c == 0:
-                for direct in range(DIRECT, CHUNKS):
-                    ocean_copy(direct, away, dy, 4 + index).start()
-
-    for step in range(CHUNKS + 1):
-        if step < CHUNKS:
-            arrived(step, 0, near)
-            pass_on(step, near, 0)
-        if step > 0:
-
-            @when_far
-            def _():
-                arrived(step - 1, 0, far)
-                pass_on(step - 1, far, 1)
-
-        if step == 1:
-            for dx, dy in AROUND:
-
-                @when(dx, dy)
-                def _():
-                    meta_copy(dx, dy).start()
-
-        if step < CHUNKS:
-            arrived(step, mate, 0)
-            acc[...] += product(mate, 0, step) + product(0, near, step)
-
-            @when_away
-            def _():
-                arrived(step, away, 0)
-                acc[...] += product(away, 0, step)
-
-        if step > 0:
-
-            @when_far
-            def _():
-                acc[...] += product(0, far, step - 1)
-
-    for c in range(CHUNKS):
-        arrived(c, mate, near)
-        acc[...] += product(mate, near, c)
-
-        @when_far
-        def _():
-            arrived(c, mate, far)
-            acc[...] += product(mate, far, c)
-
-    for c in range(CHUNKS):
-
-        @when_away
-        def _():
-            arrived(c, away, near)
-            acc[...] += product(away, near, c)
-
-            @when_far
-            def _():
-                arrived(c, away, far)
-                acc[...] += product(away, far, c)
+            corner(away, near, piece)
+            when_far(lambda: corner(away, far, piece))
 
     sst = acc[...]
     mean = jnp.sum(sst, axis=0, keepdims=True) / MEM
@@ -332,44 +338,54 @@
         pack_x[0, 8 * block : 8 * block + 8, :] = north
         pack_x[1, 8 * block : 8 * block + 8, :] = south
 
-    def halo_copy(dx, dy):
-        if dy < 0:
-            source, target = pack_y.at[0], in_w.at[1 - dx]
-        elif dy > 0:
-            source, target = pack_y.at[1], in_e.at[1 - dx]
-        elif dx < 0:
-            source, target = pack_x.at[0], in_n
-        else:
-            source, target = pack_x.at[1], in_s
+    def halo_y(dx, dy):
+        side = (dy + 1) // 2
         return pltpu.make_async_remote_copy(
-            src_ref=source,
-            dst_ref=target,
+            src_ref=pack_y.at[side],
+            dst_ref=in_y.at[side, 1 - dx],
             send_sem=halo_send.at[slot(dx, dy)],
             recv_sem=halo_recv.at[slot(-dx, -dy)],
             device_id=device(dx, dy),
             device_id_type=MESH,
         )
 
+    def halo_x(dx):
+        side = (dx + 1) // 2
+        return pltpu.make_async_remote_copy(
+            src_ref=pack_x.at[side],
+            dst_ref=in_x.at[side],
+            send_sem=halo_send.at[slot(dx, 0)],
+            recv_sem=halo_recv.at[slot(-dx, 0)],
+            device_id=device(dx, 0),
+            device_id_type=MESH,
+        )
+
+    @when_away
+    def _():
+        when_far(lambda: halo_y(away, far).start())
+        halo_y(away, near).start()
+
+    @when_far
+    def _():
+        halo_y(mate, far).start()
+        halo_y(0, far).start()
+
+    halo_y(mate, near).start()
+    halo_y(0, near).start()
+    when_away(lambda: halo_x(away).start())
+    halo_x(mate).start()
+
     f_out[0, :MEM, :] = anomaly
     f_out[0, MEM:, :] = pieces[-1]
 
-    for dx, dy in ((1, 1), (1, -1), (-1, 1), (-1, -1), (0, 1), (0, -1), (1, 0), (-1, 0)):
-
-        @when(dx, dy)
-        def _():
-            halo_copy(dx, dy).start()
-
     absent = jnp.where(lax.broadcasted_iota(jnp.int32, (8, CELLS), 0) == 2, 1.0, 0.0)
-    for dx, dy in AROUND:
-
-        @when(dx, dy)
-        def _():
-            meta_copy(-dx, -dy).wait_recv()
+    meta_copy(-mate, 0, 2).wait_recv()
+    when_away(lambda: meta_copy(-away, 0, 3).wait_recv())
 
     blocks = []
     for dx, dy in NEAR:
         if (dx, dy) == (0, 0):
-            blocks.append(meta[...])
+            blocks.append(meta_in[4])
         else:
             blocks.append(jnp.where(has(dx, dy), meta_in[slot(dx, dy)], absent))
     blocks.append(jnp.zeros((CELLS - 72, CELLS), jnp.float32))
@@ -407,40 +423,40 @@
             for n, part in enumerate(place()):
                 obs_out[batch, f, n] = part
 
-    for c in range(CHUNKS):
-        ocean_copy(c, 0, near, 0).wait_send()
-        ocean_copy(c, mate, 0, 2).wait_send()
-        relay_copy(c, mate, near, 0).wait_send()
-
-        @when_far
-        def _():
-            ocean_copy(c, 0, far, 1).wait_send()
-            relay_copy(c, mate, far, 2).wait_send()
-
-        @when_away
-        def _():
-            ocean_copy(c, away, 0, 3).wait_send()
-            for dy, index, there in ((near, 0, None), (far, 1, has_far)):
-
-                def finish():
-                    if c < DIRECT:
-                        relay_copy(c, away, dy, 2 * index + 1).wait_send()
-                    else:
-                        ocean_copy(c, away, dy, 4 + index).wait_send()
-
-                finish() if there is None else pl.when(there)(finish)
-
-    for dx, dy in AROUND:
-
-        @when(dx, dy)
-        def _():
-            meta_copy(dx, dy).wait_send()
-
-    for dx, dy in AROUND:
-
-        @when(dx, dy)
-        def _():
-            halo_copy(-dx, -dy).wait_recv()
+    def finish(far_needed, away_needed):
+        for f, a, spec in sends:
+            if (f, a) == (far_needed, away_needed):
+                ocean_copy(*spec).wait_send()
+
+    finish(False, False)
+    meta_copy(0, near, 0).wait_send()
+    meta_copy(mate, 0, 2).wait_send()
+
+    @when_far
+    def _():
+        finish(True, False)
+        meta_copy(0, far, 1).wait_send()
+
+    @when_away
+    def _():
+        finish(False, True)
+        meta_copy(away, 0, 3).wait_send()
+        when_far(lambda: finish(True, True))
+
+    halo_x(-mate).wait_recv()
+    halo_y(0, -near).wait_recv()
+    halo_y(-mate, -near).wait_recv()
+
+    @when_far
+    def _():
+        halo_y(0, -far).wait_recv()
+        halo_y(-mate, -far).wait_recv()
+
+    @when_away
+    def _():
+        halo_x(-away).wait_recv()
+        halo_y(-away, -near).wait_recv()
+        when_far(lambda: halo_y(-away, -far).wait_recv())
 
     low_y = (lane8 % AY) < 8
     low_x = lane8 < 64
@@ -449,13 +465,13 @@
     def present(ref, dx, dy):
         return jnp.where(has(dx, dy), ref[...], 0.0)
 
-    north = present(in_n, 1, 0)
-    south = present(in_s, -1, 0)
-    west = present(in_w.at[1], 0, 1)
-    east = present(in_e.at[1], 0, -1)
+    north = present(in_x.at[0], 1, 0)
+    south = present(in_x.at[1], -1, 0)
+    west = present(in_y.at[0, 1], 0, 1)
+    east = present(in_y.at[1, 1], 0, -1)
     low16 = lax.broadcasted_iota(jnp.int32, (16, CELLS), 1) < 64
-    west_c = jnp.where(low16, present(in_w.at[2], 1, 1), present(in_w.at[0], -1, 1))
-    east_c = jnp.where(low16, present(in_e.at[2], 1, -1), present(in_e.at[0], -1, -1))
+    west_c = jnp.where(low16, present(in_y.at[0, 2], 1, 1), present(in_y.at[0, 0], -1, 1))
+    east_c = jnp.where(low16, present(in_y.at[1, 2], 1, -1), present(in_y.at[1, 0], -1, -1))
     for g in range(GROUPS):
         at = pl.ds(8 * g, 8)
         b, s = g // 4, g % 4
@@ -472,11 +488,20 @@
                 roll(e[8 * b : 8 * b + 8], 2 * s),
             )
 
-    for dx, dy in AROUND:
-
-        @when(dx, dy)
-        def _():
-            halo_copy(dx, dy).wait_send()
+    halo_x(mate).wait_send()
+    halo_y(0, near).wait_send()
+    halo_y(mate, near).wait_send()
+
+    @when_far
+    def _():
+        halo_y(0, far).wait_send()
+        halo_y(mate, far).wait_send()
+
+    @when_away
+    def _():
+        halo_x(away).wait_send()
+        halo_y(away, near).wait_send()
+        when_far(lambda: halo_y(away, far).wait_send())
 
 
 def update_kernel(
@@ -675,19 +700,15 @@
             pltpu.VMEM((K, OCN_DEV, CELLS), jnp.bfloat16),
             pltpu.VMEM((MEM, CELLS), f32),
             pltpu.VMEM((CELLS, CELLS), f32),
-            pltpu.VMEM((8, CELLS), f32),
             pltpu.VMEM((9, 8, CELLS), f32),
             pltpu.VMEM((2, 16, CELLS), f32),
             pltpu.VMEM((2, 24, CELLS), f32),
-            pltpu.VMEM((3, 16, CELLS), f32),
-            pltpu.VMEM((3, 16, CELLS), f32),
-            pltpu.VMEM((24, CELLS), f32),
-            pltpu.VMEM((24, CELLS), f32),
+            pltpu.VMEM((2, 3, 16, CELLS), f32),
+            pltpu.VMEM((2, 24, CELLS), f32),
             dma((CHUNKS + 7,)),
+            dma((24,)),
             dma((9, CHUNKS)),
-            dma((9, CHUNKS)),
-            dma((9, CHUNKS)),
-            dma((9,)),
+            dma((4,)),
             dma((9,)),
             dma((9,)),
             dma((9,)),

time: 24.3 us -> 23.7 us (0.975); the launches traced: 24.2 us -> 23.3 us
  Pallas kernels: 23.5 us -> 22.7 us
    pallas_call x1, Pallas kernels: 19.2 us -> 18.3 us  [local(): pl.pallas_call(exchange_kernel, out_shape=(jax.ShapeDtypeStruct((4, ROWS,...]
where the time goes in v3:
time: 23.7 us; the launch traced here: 23.3 us
  Pallas kernels  22.7 us (96%)
  between operations  0.66 us (3%)
    pallas_call x1, Pallas kernels, local(): pl.pallas_call(exchange_kernel, out_shape=(jax.ShapeDtypeStruct((4, ROWS,...  18.3 us
    pallas_call x1, Pallas kernels, local(): pl.pallas_call(update_kernel, out_shape=(jax.ShapeDtypeStruct((COMP, 1, C...  4.35 us

profile of v3, /device:TPU:7, one launch (start us, length us, event | category | flops | bytes accessed | tf_op | source)
XLA Modules:
  0.0 23.3 jit_solution(9359583448375672526)
XLA Ops:
  0.6 0.0 copy-start
  0.6 18.3 %shard_map.104 = (f32[4,88,128]{2,1,0:T(8,128)S(1)}, f32[2,4,4,32,128]{4,3,2,1,0:T(8,128)S(1)}) custom-call(s32[1,4]{1,0:T(1,128)} %bitcast.20, bf16[80,1024]{1,0:T(8,128)(2,1)} %bitcast.19, bf16[4,1024,128]{2,1,0:T(8,128)(2,1)} %bitcast.18, s32[1,64]{1,0:T(1,128)} %bitcast.21, f32[1,64]{1,0:T(1,128)} %bitcast.22, f32[1,64]{1,0:T(1,128)} %bitcast.23, ...), custom_call_target="tpu_custom_call" | custom-call | tf_op jit(solution)/shard_map/pallas_call | solution.py:687
  19.0 0.0 copy-done
  19.0 4.3 %shard_map.105 = (f32[13,1,128]{2,1,0:T(1,128)}, f32[13,80,128]{2,1,0:T(8,128)}) custom-call(f32[4,88,128]{2,1,0:T(8,128)S(1)} %get-tuple-element.6.f_in, f32[2,4,4,32,128]{4,3,2,1,0:T(8,128)S(1)} %get-tuple-element.7.obs, f32[12,80,128]{2,1,0:T(8,128)S(1)} %bitcast.17), custom_call_target="tpu_custom_call" | custom-call | tf_op jit(solution)/shard_map/pallas_call | solution.py:734
Async XLA Ops:
  0.6 18.3 %copy-start = (f32[1,1,80,12,128]{4,2,3,1,0:T(8,128)S(1)}, f32[1,1,80,12,128]{4,2,3,1,0:T(8,128)}, u32[]{:S(2)}) copy-start(f32[1,1,80,12,128]{4,2,3,1,0:T(8,128)} %param.9) | copy-start | bytes 1474564

commit v4 on v3

--- a/solution.py
+++ b/solution.py
@@ -2,6 +2,7 @@
 
 import jax
 import jax.numpy as jnp
+import numpy as np
 from jax import lax
 from jax.experimental import pallas as pl
 from jax.experimental.pallas import tpu as pltpu
@@ -29,6 +30,44 @@
 AROUND = [d for d in NEAR if d != (0, 0)]
 
 
+def build_tables():
+    ring_e, ring_r, gathered = {}, {}, np.zeros(CELLS, np.int32)
+    middle = {0: 32, 1: 64}
+    for x in range(-2, AX + 2):
+        for y in range(-2, AY + 2):
+            out_x, out_y = not 0 <= x < AX, not 0 <= y < AY
+            if not (out_x or out_y):
+                continue
+            lane = (x % AX) * AY + y % AY
+            if out_y:
+                gathered[middle[out_x]] = lane
+                lane = middle[out_x]
+                middle[out_x] += 1
+            ring_e[x, y] = lane
+            if -1 <= x <= AX and -1 <= y <= AY:
+                ring_r[x, y] = len(ring_r)
+
+    def code(x, y, ring):
+        inside = 0 <= x < AX and 0 <= y < AY
+        return x * AY + y if inside else CELLS + ring[x, y]
+
+    shifts = np.zeros((28, CELLS), np.int32)
+    for d, (dx, dy) in enumerate(NEAR):
+        for c in range(CELLS):
+            x, y = c // AY + dx, c % AY + dy
+            shifts[d, c] = code(x, y, ring_e)
+            shifts[18 + d, c] = code(x, y, ring_r)
+        for (x, y), lane in ring_r.items():
+            shifts[9 + d, lane] = code(x + dx, y + dy, ring_e)
+    shifts[27] = gathered
+    owners = np.full((8, CELLS), -1, np.int32)
+    for n, ring in enumerate((ring_e, ring_r)):
+        for (x, y), lane in ring.items():
+            owners[2 * n, lane] = (x % AX) * AY + y % AY
+            owners[2 * n + 1, lane] = slot(x // AX, y // AY)
+    return np.repeat(shifts[:, None], 8, axis=1), owners
+
+
 def slot(dx, dy):
     return (dx + 1) * 3 + dy + 1
 
@@ -47,9 +86,11 @@
     error_hbm,
     live_hbm,
     order_hbm,
+    owners_hbm,
     f_out,
     obs_out,
     src,
+    owners,
     ints,
     floats,
     oce,
@@ -195,6 +236,7 @@
                 (value_hbm, floats.at[0]),
                 (error_hbm, floats.at[1]),
                 (src_hbm, src),
+                (owners_hbm, owners),
             )
         )
     ]
@@ -392,12 +434,10 @@
     columns[...] = jnp.concatenate(blocks, axis=0).T
 
     lane32 = lax.broadcasted_iota(jnp.int32, (OB, CELLS), 1)
-    lanes = lane32.astype(jnp.float32)
-    low_x32, low_y32 = lane32 < 64, (lane32 % AY) < 8
     for batch in range(NB):
         rows = slice(batch * OB, (batch + 1) * OB)
 
-        def dense(dx, dy):
+        def dense(dx, dy, lanes):
             at = 8 * slot(dx, dy)
             cells, values, errors, alive = (
                 jnp.broadcast_to(columns[rows, at + n : at + n + 1], (OB, CELLS))
@@ -406,22 +446,17 @@
             hit = jnp.where(cells == lanes, alive, 0.0)
             return hit, hit * values, errors + (1.0 - alive), errors
 
-        def either(mask, first, second):
-            return tuple(jnp.where(mask, a, b) for a, b in zip(first, second))
-
-        places = [
-            lambda: dense(0, 0),
-            lambda: either(low_x32, dense(1, 0), dense(-1, 0)),
-            lambda: either(low_y32, dense(0, 1), dense(0, -1)),
-            lambda: either(
-                low_y32,
-                either(low_x32, dense(1, 1), dense(-1, 1)),
-                either(low_x32, dense(1, -1), dense(-1, -1)),
-            ),
-        ]
-        for f, place in enumerate(places):
-            for n, part in enumerate(place()):
-                obs_out[batch, f, n] = part
+        cell_row = jnp.broadcast_to(owners[2 * batch : 2 * batch + 1, :], (OB, CELLS))
+        tile_row = jnp.broadcast_to(owners[2 * batch + 1 : 2 * batch + 2, :], (OB, CELLS))
+        cell_row = cell_row.astype(jnp.float32)
+        around = dense(-1, -1, cell_row)
+        for dx, dy in AROUND[1:]:
+            other = dense(dx, dy, cell_row)
+            chosen = tile_row == slot(dx, dy)
+            around = tuple(jnp.where(chosen, n, o) for n, o in zip(other, around))
+        for place, parts in enumerate((dense(0, 0, lane32.astype(jnp.float32)), around)):
+            for n, part in enumerate(parts):
+                obs_out[batch, place, n] = part
 
     def finish(far_needed, away_needed):
         for f, a, spec in sends:
@@ -507,42 +542,42 @@
 def update_kernel(
     f_in,
     obs,
+    tables,
     atm,
     mean_out,
     anom_out,
+    around,
     state,
-    shifted,
+    first_shifts,
+    other_shifts,
+    second_shifts,
     factors,
+    covariance,
     result,
+    field_mean,
     means,
     out_sem,
     mean_sem,
 ):
     lane8 = lax.broadcasted_iota(jnp.int32, (8, CELLS), 1)
-    y8 = lane8 % AY
-    first_y, last_y = y8 == 0, y8 == AY - 1
-    first_x, last_x = lane8 < AY, lane8 >= CELLS - AY
     groups = range(MEM // 8)
+    pairs = FIELDS // 2
+    always = lax.axis_index("gx") >= 0
 
     def at(g):
         return slice(8 * g, 8 * g + 8)
 
-    def shift_all(blocks, wanted):
-        out = {}
-        turned = {}
-        for f in range(4):
-            if any((f ^ a) in wanted for a in (0, 1)):
-                other = blocks[f ^ 2]
-                turned[f, 0] = blocks[f]
-                turned[f, 1] = jnp.where(last_y, roll(other, 15), roll(blocks[f], -1))
-                turned[f, -1] = jnp.where(first_y, roll(other, -15), roll(blocks[f], 1))
-        for f in wanted:
-            for dy in (-1, 0, 1):
-                own, other = turned[f, dy], turned[f ^ 1, dy]
-                out[f, slot(0, dy)] = own
-                out[f, slot(1, dy)] = roll(jnp.where(first_x, other, own), -AY)
-                out[f, slot(-1, dy)] = roll(jnp.where(last_x, other, own), AY)
-        return out
+    def take(block, lanes):
+        return jnp.take_along_axis(block, lanes, axis=1, mode="promise_in_bounds")
+
+    def shift(base, d, own, ring):
+        if d == 4 and base != 9:
+            return own
+        table = tables[base + d]
+        lanes = jnp.bitwise_and(table, CELLS - 1)
+        if d == 4:
+            return take(ring, lanes)
+        return jnp.where(table >= CELLS, take(ring, lanes), take(own, lanes))
 
     def allsum(x):
         for step in (4, 2, 1):
@@ -554,16 +589,12 @@
         max(1.0 - (dx * dx + dy * dy) / 4.0, 0.0) ** 2 / (MEM - 1) for dx, dy in NEAR
     ]
 
-    for batch in range(NB):
-        source = f_in if batch == 0 else state
-        wanted = (0, 1, 2, 3) if batch == 0 else (0,)
-        base = 0 if batch == 0 else 36
-
+    def observe(batch, sources, bases):
         alphas, betas = [], []
-        for f in range(4):
+        for f, source in enumerate(sources):
             square = zero
             for g in groups:
-                block = source[f, at(g), :]
+                block = source[at(g), :]
                 square = square + block * block
             variance = allsum(square) / (MEM - 1)
             total = [zero, zero, zero]
@@ -578,93 +609,127 @@
                 total[1] = total[1] + weighting
                 total[2] = total[2] + masked_value * inverse
             betas.append(allsum(total[0]))
-            alphas.append(allsum(total[2]) - source[f, MEM:, :] * allsum(total[1]))
-        alphas = shift_all(alphas, wanted)
-        betas = shift_all(betas, wanted)
-        alphas = {key: alphas[key] * tapers[key[1]] for key in alphas}
-        betas = {key: betas[key] * tapers[key[1]] for key in betas}
+            alphas.append(allsum(total[2]) - source[MEM:, :] * allsum(total[1]))
+        for base in bases:
+            for kind, blocks in enumerate((alphas, betas)):
+                for d in range(9):
+                    factors[kind, base + d] = shift(base, d, *blocks) * tapers[d]
+
+    def shift_groups(base, target, own, ring, chosen):
+        for g in chosen:
+            for d in range(9):
+                target[d, at(g), :] = shift(base, d, own[at(g), :], ring[at(g), :])
+
+    def sst_step(base, source, mean, shifts, store):
+        sums = [zero] * 9
+        for g in groups:
+            block = source[at(g), :]
+            for d in range(9):
+                sums[d] = sums[d] + shifts[d, at(g), :] * block
+        sums = [allsum(x) for x in sums]
         for d in range(9):
-            factors[batch, 0, d] = alphas[0, d]
-            factors[batch, 1, d] = betas[0, d]
-
+            mean = mean + factors[0, base + d] * sums[d]
+        gains = [factors[1, base + d] * sums[d] for d in range(9)]
         for g in groups:
-            moved = shift_all([source[f, at(g), :] for f in range(4)], wanted)
-            for f in wanted:
+            block = source[at(g), :]
+            for d in range(9):
+                block = block - shifts[d, at(g), :] * gains[d]
+            store[at(g), :] = block
+        return mean
+
+    def field_step(base, shifted, fields, sums):
+        mean = [field_mean[u] for u in fields]
+        for n, u in enumerate(fields):
+            for d in range(9):
+                mean[n] = mean[n] + factors[0, base + d] * sums[n][d]
+        gains = [[factors[1, base + d] * sums[n][d] for d in range(9)] for n in range(2)]
+        for g in groups:
+            for n, u in enumerate(fields):
+                block = result[u, at(g), :]
                 for d in range(9):
-                    shifted[base + 9 * f + d, at(g), :] = moved[f, d]
-
-        for f in wanted:
-            sums = [zero] * 9
-            for g in groups:
-                block = source[f, at(g), :]
+                    block = block - shifted[d, at(g), :] * gains[n][d]
+                result[u, at(g), :] = block
+        return mean
+
+    gathered = tables[27]
+    edge = jnp.logical_or(lane8 < 32, lane8 >= 96)
+    for g in range(GROUPS):
+        middle = jnp.where(
+            lane8 < 64, take(f_in[2, at(g), :], gathered), take(f_in[3, at(g), :], gathered)
+        )
+        around[at(g), :] = jnp.where(edge, f_in[1, at(g), :], middle)
+    own = f_in.at[0]
+    shift_groups(0, first_shifts, own, around, groups)
+    observe(0, (own, around), (0, 9))
+
+    def first_covariance(pair):
+        fields = (2 * pair, 2 * pair + 1)
+        total = [zero, zero]
+        for g in groups:
+            for n, u in enumerate(fields):
+                total[n] = total[n] + atm[u, at(g), :]
+        mean = [allsum(x) / MEM for x in total]
+        sums = [[zero] * 9, [zero] * 9]
+        for g in groups:
+            for n, u in enumerate(fields):
+                block = atm[u, at(g), :] - mean[n]
+                result[u, at(g), :] = block
                 for d in range(9):
-                    sums[d] = sums[d] + shifted[base + 9 * f + d, at(g), :] * block
-            sums = [allsum(x) for x in sums]
-            mean = source[f, MEM:, :]
+                    sums[n][d] = sums[n][d] + first_shifts[d, at(g), :] * block
+        for n, u in enumerate(fields):
+            field_mean[u] = mean[n]
             for d in range(9):
-                mean = mean + alphas[f, d] * sums[d]
-            gains = [betas[f, d] * sums[d] for d in range(9)]
-            for g in groups:
-                block = source[f, at(g), :]
-                for d in range(9):
-                    block = block - shifted[base + 9 * f + d, at(g), :] * gains[d]
-                if batch + 1 < NB:
-                    state[f, at(g), :] = block
-                else:
-                    result[FIELDS, at(g), :] = block
-            if batch + 1 < NB:
-                state[f, MEM:, :] = mean
-            else:
-                means[FIELDS] = mean[:1]
-
-    def sst_copy():
-        return pltpu.make_async_copy(result.at[FIELDS], anom_out.at[FIELDS], mean_sem.at[1])
+                covariance[u, d] = allsum(sums[n][d])
+        shift_groups(9, other_shifts, own, around, groups[2 * pair : 2 * pair + 2])
+
+    for pair in range(pairs):
+        pl.when(always)(functools.partial(first_covariance, pair))
+    state[0, MEM:, :] = sst_step(0, own, own[MEM:, :], first_shifts, state.at[0])
+    mean = shift(9, 4, own[MEM:, :], around[MEM:, :])
+    state[1, MEM:, :] = sst_step(9, other_shifts.at[4], mean, other_shifts, state.at[1])
+    observe(1, (state.at[0], state.at[1]), (18,))
+
+    def first_update(pair):
+        fields = (2 * pair, 2 * pair + 1)
+        sums = [[covariance[u, d] for d in range(9)] for u in fields]
+        mean = field_step(0, first_shifts, fields, sums)
+        for n, u in enumerate(fields):
+            field_mean[u] = mean[n]
+        shift_groups(
+            18, second_shifts, state.at[0], state.at[1], groups[2 * pair : 2 * pair + 2]
+        )
+
+    for pair in range(pairs):
+        pl.when(always)(functools.partial(first_update, pair))
+    mean = sst_step(18, state.at[0], state[0, MEM:, :], second_shifts, result.at[FIELDS])
+    means[FIELDS] = mean[:1]
+    sst_copy = pltpu.make_async_copy(result.at[FIELDS], anom_out.at[FIELDS], mean_sem.at[1])
+    sst_copy.start()
 
     def field_copy(pair):
         part = pl.ds(2 * pair, 2)
         return pltpu.make_async_copy(result.at[part], anom_out.at[part], out_sem.at[pair])
 
-    sst_copy().start()
-
-    def two_fields(pair, carry):
+    def second_batch(pair):
         fields = (2 * pair, 2 * pair + 1)
-        sums = [zero, zero]
+        sums = [[zero] * 9, [zero] * 9]
         for g in groups:
-            for u in range(2):
-                sums[u] = sums[u] + atm[fields[u], at(g), :]
-        mean = [allsum(x) / MEM for x in sums]
-        for batch in range(NB):
-            sums = [[zero] * 9, [zero] * 9]
-            for g in groups:
-                for u in range(2):
-                    if batch == 0:
-                        block = atm[fields[u], at(g), :] - mean[u]
-                        result[fields[u], at(g), :] = block
-                    else:
-                        block = result[fields[u], at(g), :]
-                    for d in range(9):
-                        sums[u][d] = sums[u][d] + shifted[36 * batch + d, at(g), :] * block
-            sums = [[allsum(x) for x in sums[u]] for u in range(2)]
-            for u in range(2):
+            for n, u in enumerate(fields):
+                block = result[u, at(g), :]
                 for d in range(9):
-                    mean[u] = mean[u] + factors[batch, 0, d] * sums[u][d]
-            gains = [[factors[batch, 1, d] * sums[u][d] for d in range(9)] for u in range(2)]
-            for g in groups:
-                for u in range(2):
-                    block = result[fields[u], at(g), :]
-                    for d in range(9):
-                        block = block - shifted[36 * batch + d, at(g), :] * gains[u][d]
-                    result[fields[u], at(g), :] = block
-        for u in range(2):
-            means[fields[u]] = mean[u][:1]
+                    sums[n][d] = sums[n][d] + second_shifts[d, at(g), :] * block
+        sums = [[allsum(x) for x in sums[n]] for n in range(2)]
+        mean = field_step(18, second_shifts, fields, sums)
+        for n, u in enumerate(fields):
+            means[u] = mean[n][:1]
         field_copy(pair).start()
-        return carry
-
-    lax.fori_loop(0, FIELDS // 2, two_fields, 0)
+
+    for pair in range(pairs):
+        pl.when(always)(functools.partial(second_batch, pair))
     mean_copy = pltpu.make_async_copy(means, mean_out, mean_sem.at[0])
     mean_copy.start()
-    sst_copy().wait()
-    for pair in range(FIELDS // 2):
+    sst_copy.wait()
+    for pair in range(pairs):
         field_copy(pair).wait()
     mean_copy.wait()
 
@@ -681,19 +746,21 @@
     obs_order,
 ):
     f32 = jnp.float32
+    shifts, owners = build_tables()
     vmem = pl.BlockSpec(memory_space=pltpu.VMEM)
     hbm = pl.BlockSpec(memory_space=pltpu.HBM)
     dma = pltpu.SemaphoreType.DMA
-    state, meta = pl.pallas_call(
+    state, tables = pl.pallas_call(
         exchange_kernel,
         out_shape=(
             jax.ShapeDtypeStruct((4, ROWS, CELLS), f32),
-            jax.ShapeDtypeStruct((NB, 4, 4, OB, CELLS), f32),
+            jax.ShapeDtypeStruct((NB, 2, 4, OB, CELLS), f32),
         ),
-        in_specs=[hbm] * 8,
+        in_specs=[hbm] * 9,
         out_specs=(vmem, vmem),
         scratch_shapes=[
             pltpu.SMEM((1, K), jnp.int32),
+            pltpu.VMEM((8, CELLS), jnp.int32),
             pltpu.VMEM((3, 1, OBS), jnp.int32),
             pltpu.VMEM((2, 1, OBS), f32),
             pltpu.VMEM((9, CHUNKS, MEM, CW), jnp.bfloat16),
@@ -705,7 +772,7 @@
             pltpu.VMEM((2, 24, CELLS), f32),
             pltpu.VMEM((2, 3, 16, CELLS), f32),
             pltpu.VMEM((2, 24, CELLS), f32),
-            dma((CHUNKS + 7,)),
+            dma((CHUNKS + 8,)),
             dma((24,)),
             dma((9, CHUNKS)),
             dma((4,)),
@@ -728,6 +795,7 @@
                 obs_error[0],
                 obs_live[0],
                 obs_order[0],
+                jnp.asarray(owners),
             )
         )
     )
@@ -737,19 +805,24 @@
             jax.ShapeDtypeStruct((COMP, 1, CELLS), f32),
             jax.ShapeDtypeStruct((COMP, MEM, CELLS), f32),
         ),
-        in_specs=[vmem] * 3,
+        in_specs=[vmem] * 4,
         out_specs=(hbm, hbm),
         scratch_shapes=[
-            pltpu.VMEM((4, ROWS, CELLS), f32),
-            pltpu.VMEM((45, MEM, CELLS), f32),
-            pltpu.VMEM((NB, 2, 9, 8, CELLS), f32),
+            pltpu.VMEM((ROWS, CELLS), f32),
+            pltpu.VMEM((2, ROWS, CELLS), f32),
+            pltpu.VMEM((9, MEM, CELLS), f32),
+            pltpu.VMEM((9, MEM, CELLS), f32),
+            pltpu.VMEM((9, MEM, CELLS), f32),
+            pltpu.VMEM((2, 27, 8, CELLS), f32),
+            pltpu.VMEM((FIELDS, 9, 8, CELLS), f32),
             pltpu.VMEM((COMP, MEM, CELLS), f32),
+            pltpu.VMEM((FIELDS, 8, CELLS), f32),
             pltpu.VMEM((COMP, 1, CELLS), f32),
             dma((FIELDS // 2,)),
             dma((2,)),
         ],
         compiler_params=pltpu.CompilerParams(vmem_limit_bytes=16 * 1024 * 1024),
-    )(state, meta, jnp.transpose(atm_members[0, 0], (1, 0, 2)))
+    )(state, tables, jnp.asarray(shifts), jnp.transpose(atm_members[0, 0], (1, 0, 2)))
     return (mean.reshape(1, 1, COMP, CELLS), jnp.transpose(anomaly, (1, 0, 2))[None, None])
 
 

time: 23.7 us -> 23.4 us (0.987)
  Pallas kernels: 22.7 us -> 22.3 us
    pallas_call x1, Pallas kernels: 4.35 us -> 3.95 us  [local(): pl.pallas_call(update_kernel, out_shape=(jax.ShapeDtypeStruct((COMP, 1, C...]
where the time goes in v4:
time: 23.4 us; the launch traced here: 23 us
  Pallas kernels  22.3 us (95%)
  between operations  0.67 us (3%)
    pallas_call x1, Pallas kernels, local(): pl.pallas_call(exchange_kernel, out_shape=(jax.ShapeDtypeStruct((4, ROWS,...  18.3 us
    pallas_call x1, Pallas kernels, local(): pl.pallas_call(update_kernel, out_shape=(jax.ShapeDtypeStruct((COMP, 1, C...  3.95 us

profile of v4, /device:TPU:7, one launch (start us, length us, event | category | flops | bytes accessed | tf_op | source)
XLA Modules:
  0.0 23.0 jit_solution(17176366944154945268)
XLA Ops:
  0.6 0.0 copy-start
  0.6 0.0 copy-start.1
  0.7 18.3 %shard_map.122 = (f32[4,88,128]{2,1,0:T(8,128)S(1)}, f32[2,2,4,32,128]{4,3,2,1,0:T(8,128)S(1)}) custom-call(s32[1,4]{1,0:T(1,128)} %bitcast.20, bf16[80,1024]{1,0:T(8,128)(2,1)} %bitcast.19, bf16[4,1024,128]{2,1,0:T(8,128)(2,1)} %bitcast.18, s32[1,64]{1,0:T(1,128)} %bitcast.21, f32[1,64]{1,0:T(1,128)} %bitcast.22, f32[1,64]{1,0:T(1,128)} %bitcast.23, ...), custom_call_target="tpu_custom_call" | custom-call | tf_op jit(solution)/shard_map/pallas_call | solution.py:753
  19.0 0.0 copy-done
  19.0 0.0 copy-done.1
  19.0 3.9 %shard_map.123 = (f32[13,1,128]{2,1,0:T(1,128)}, f32[13,80,128]{2,1,0:T(8,128)}) custom-call(f32[4,88,128]{2,1,0:T(8,128)S(1)} %get-tuple-element.6.f_in, f32[2,2,4,32,128]{4,3,2,1,0:T(8,128)S(1)} %get-tuple-element.7.obs, s32[28,8,128]{2,1,0:T(8,128)S(1)} %copy-done.1, f32[12,80,128]{2,1,0:T(8,128)S(1)} %bitcast.17), custom_call_target="tpu_custom_call" | custom-call | tf_op jit(solution)/shard_map/pallas_call | solution.py:802
Async XLA Ops:
  0.6 18.4 %copy-start = (f32[1,1,80,12,128]{4,2,3,1,0:T(8,128)S(1)}, f32[1,1,80,12,128]{4,2,3,1,0:T(8,128)}, u32[]{:S(2)}) copy-start(f32[1,1,80,12,128]{4,2,3,1,0:T(8,128)} %param.11) | copy-start | bytes 1474564
  0.6 18.4 %copy-start.1 = (s32[28,8,128]{2,1,0:T(8,128)S(1)}, s32[28,8,128]{2,1,0:T(8,128)}, u32[]{:S(2)}) copy-start(s32[28,8,128]{2,1,0:T(8,128)} %constant.5.clone.tables) | copy-start | bytes 344068

commit v5 on v4

--- a/solution.py
+++ b/solution.py
@@ -40,7 +40,7 @@
                 continue
             lane = (x % AX) * AY + y % AY
             if out_y:
-                gathered[middle[out_x]] = lane
+                gathered[middle[out_x]] = (lane + 4 * out_x) % CELLS
                 lane = middle[out_x]
                 middle[out_x] += 1
             ring_e[x, y] = lane
@@ -72,6 +72,10 @@
     return (dx + 1) * 3 + dy + 1
 
 
+def home(dx, dy):
+    return (dx + 1) * 3 + (2 if isinstance(dy, int) and dy == 0 else (dy + 1) // 2)
+
+
 def roll(x, shift):
     shift = shift % CELLS
     return x if shift == 0 else pltpu.roll(x, shift, 1)
@@ -88,6 +92,7 @@
     order_hbm,
     owners_hbm,
     f_out,
+    own_shifts,
     obs_out,
     src,
     owners,
@@ -105,6 +110,8 @@
     local_sem,
     oce_send,
     oce_recv,
+    both_send,
+    both_recv,
     meta_send,
     meta_recv,
     halo_send,
@@ -122,6 +129,7 @@
     far = -near
     has_far = jnp.logical_and(j + far >= 0, j + far < ny)
     when_away, when_far = pl.when(has_away), pl.when(has_far)
+    when_no_far = pl.when(jnp.logical_not(has_far))
 
     def has(dx, dy):
         cond = None
@@ -139,7 +147,7 @@
 
     own_load = [
         pltpu.make_async_copy(
-            ocean.at[:, pl.ds(c * CW, CW)], oce.at[4, c], local_sem.at[c]
+            ocean.at[:, pl.ds(c * CW, CW)], oce.at[home(0, 0), c], local_sem.at[c]
         )
         for c in range(CHUNKS)
     ]
@@ -172,9 +180,9 @@
         return oce.at[p, pl.ds(*piece)]
 
     def ocean_copy(piece, from_dx, from_dy, dx, dy, sem):
-        target = slot(from_dx - dx, from_dy - dy)
+        target = home(from_dx - dx, from_dy - dy)
         return pltpu.make_async_remote_copy(
-            src_ref=tile(slot(from_dx, from_dy), piece),
+            src_ref=tile(home(from_dx, from_dy), piece),
             dst_ref=tile(target, piece),
             send_sem=oce_send.at[sem],
             recv_sem=oce_recv.at[target, piece[0]],
@@ -184,6 +192,17 @@
 
     def arrived(piece, dx, dy):
         ocean_copy(piece, 0, 0, -dx, -dy, 0).wait_recv()
+
+    def both_copy(piece, dx, sem):
+        target = home(-dx, -1)
+        return pltpu.make_async_remote_copy(
+            src_ref=oce.at[pl.ds(home(0, -1), 2), pl.ds(*piece)],
+            dst_ref=oce.at[pl.ds(target, 2), pl.ds(*piece)],
+            send_sem=both_send.at[sem],
+            recv_sem=both_recv.at[sem],
+            device_id=device(dx, 0),
+            device_id_type=MESH,
+        )
 
     def meta_copy(dx, dy, sem):
         if isinstance(dx, int):
@@ -281,7 +300,7 @@
             which = jnp.where(positions[k] == p, k, which)
             valid = jnp.logical_or(valid, positions[k] == p)
         part = jnp.dot(
-            oce[p, c],
+            oce[home(dx, dy), c],
             wv[which, pl.ds(c * CW, CW), :],
             preferred_element_type=jnp.float32,
         )
@@ -301,11 +320,15 @@
         def one(dy, is_far):
             arrived(piece, 0, dy)
             send(is_far, False, piece, 0, dy, mate, 0)
-            if with_away:
-                when_away(lambda: send(is_far, True, piece, 0, dy, away, 0))
 
         one(near, False)
         when_far(lambda: one(far, True))
+        if with_away:
+
+            @when_away
+            def _():
+                when_far(lambda: both_copy(piece, away, piece[0]).start())
+                when_no_far(lambda: send(None, True, piece, 0, near, away, 0))
 
     from_y(FIRST, True)
     meta_copy(0, near, 0).start()
@@ -345,12 +368,20 @@
         corner(mate, near, piece)
         when_far(lambda: corner(mate, far, piece))
 
-    for piece in (FIRST, SECOND, THIRD):
-
-        @when_away
-        def _():
-            corner(away, near, piece)
-            when_far(lambda: corner(away, far, piece))
+    @when_away
+    def _():
+        for piece in (FIRST, SECOND):
+
+            @when_far
+            def _():
+                both_copy(piece, -away, piece[0]).wait_recv()
+                add(away, near, piece)
+                add(away, far, piece)
+
+            when_no_far(lambda: corner(away, near, piece))
+
+        corner(away, near, THIRD)
+        when_far(lambda: corner(away, far, THIRD))
 
     sst = acc[...]
     mean = jnp.sum(sst, axis=0, keepdims=True) / MEM
@@ -366,8 +397,9 @@
         east = west
         for g in range(8 * block, min(8 * block + 8, GROUPS)):
             s = g % 8
-            west = jnp.where(pair == s, roll(pieces[g], 2 * s), west)
-            east = jnp.where(pair == 7 - s, roll(pieces[g], -2 * s), east)
+            moved = roll(pieces[g], 2 * s)
+            west = jnp.where(pair == s, moved, west)
+            east = jnp.where(pair == (s + 7) % 8, moved, east)
         pack_y[0, 8 * block : 8 * block + 8, :] = west
         pack_y[1, 8 * block : 8 * block + 8, :] = east
     for block in range(3):
@@ -375,8 +407,9 @@
         south = north
         for g in range(4 * block, min(4 * block + 4, GROUPS)):
             s = g % 4
-            north = jnp.where(quarter == s, roll(pieces[g], 32 * s), north)
-            south = jnp.where(quarter == 3 - s, roll(pieces[g], -32 * s), south)
+            moved = roll(pieces[g], 32 * s)
+            north = jnp.where(quarter == s, moved, north)
+            south = jnp.where(quarter == (s + 3) % 4, moved, south)
         pack_x[0, 8 * block : 8 * block + 8, :] = north
         pack_x[1, 8 * block : 8 * block + 8, :] = south
 
@@ -419,6 +452,9 @@
 
     f_out[0, :MEM, :] = anomaly
     f_out[0, MEM:, :] = pieces[-1]
+    for dx, dy in AROUND:
+        for g in range(MEM // 8):
+            own_shifts[slot(dx, dy), 8 * g : 8 * g + 8, :] = roll(pieces[g], -(AY * dx + dy))
 
     absent = jnp.where(lax.broadcasted_iota(jnp.int32, (8, CELLS), 0) == 2, 1.0, 0.0)
     meta_copy(-mate, 0, 2).wait_recv()
@@ -476,7 +512,13 @@
     def _():
         finish(False, True)
         meta_copy(away, 0, 3).wait_send()
-        when_far(lambda: finish(True, True))
+        when_no_far(lambda: finish(None, True))
+
+        @when_far
+        def _():
+            finish(True, True)
+            for piece in (FIRST, SECOND):
+                both_copy(piece, away, piece[0]).wait_send()
 
     halo_x(-mate).wait_recv()
     halo_y(0, -near).wait_recv()
@@ -492,10 +534,6 @@
         halo_x(-away).wait_recv()
         halo_y(-away, -near).wait_recv()
         when_far(lambda: halo_y(-away, -far).wait_recv())
-
-    low_y = (lane8 % AY) < 8
-    low_x = lane8 < 64
-    zero = jnp.zeros((8, CELLS), jnp.float32)
 
     def present(ref, dx, dy):
         return jnp.where(has(dx, dy), ref[...], 0.0)
@@ -504,24 +542,28 @@
     south = present(in_x.at[1], -1, 0)
     west = present(in_y.at[0, 1], 0, 1)
     east = present(in_y.at[1, 1], 0, -1)
-    low16 = lax.broadcasted_iota(jnp.int32, (16, CELLS), 1) < 64
-    west_c = jnp.where(low16, present(in_y.at[0, 2], 1, 1), present(in_y.at[0, 0], -1, 1))
-    east_c = jnp.where(low16, present(in_y.at[1, 2], 1, -1), present(in_y.at[1, 0], -1, -1))
+    corners = (
+        present(in_y.at[0, 2], 1, 1),
+        present(in_y.at[0, 0], -1, 1),
+        present(in_y.at[1, 2], 1, -1),
+        present(in_y.at[1, 0], -1, -1),
+    )
+    y8 = lane8 % AY
+    beside = jnp.logical_or(y8 < 2, y8 >= AY - 2)
     for g in range(GROUPS):
         at = pl.ds(8 * g, 8)
-        b, s = g // 4, g % 4
-        f_out[1, at, :] = jnp.where(
-            low_x,
-            roll(north[8 * b : 8 * b + 8], -32 * s),
-            roll(south[8 * b : 8 * b + 8], 32 * s),
-        )
-        b, s = g // 8, g % 8
-        for place, w, e in ((2, west, east), (3, west_c, east_c)):
-            f_out[place, at, :] = jnp.where(
-                low_y,
-                roll(w[8 * b : 8 * b + 8], -2 * s),
-                roll(e[8 * b : 8 * b + 8], 2 * s),
-            )
+        b, s = slice(8 * (g // 4), 8 * (g // 4) + 8), g % 4
+        f_out[1, at, :] = roll(jnp.where(quarter == s, north[b], south[b]), -32 * s)
+        b, s = slice(8 * (g // 8), 8 * (g // 8) + 8), g % 8
+        from_west = pair == s
+        sides = roll(jnp.where(from_west, west[b], east[b]), -2 * s)
+        low_x = jnp.logical_and(lane8 >= 2 * s, lane8 < 64 + 2 * s)
+        corner = jnp.where(
+            from_west,
+            jnp.where(low_x, corners[0][b], corners[1][b]),
+            jnp.where(low_x, corners[2][b], corners[3][b]),
+        )
+        f_out[2, at, :] = jnp.where(beside, sides, roll(corner, 4 - 2 * s))
 
     halo_x(mate).wait_send()
     halo_y(0, near).wait_send()
@@ -541,6 +583,7 @@
 
 def update_kernel(
     f_in,
+    own_shifts,
     obs,
     tables,
     atm,
@@ -562,7 +605,10 @@
     lane8 = lax.broadcasted_iota(jnp.int32, (8, CELLS), 1)
     groups = range(MEM // 8)
     pairs = FIELDS // 2
-    always = lax.axis_index("gx") >= 0
+
+    def region(n):
+        return pl.when(lax.axis_index("gx") > -1 - n)
+
 
     def at(g):
         return slice(8 * g, 8 * g + 8)
@@ -654,36 +700,51 @@
     gathered = tables[27]
     edge = jnp.logical_or(lane8 < 32, lane8 >= 96)
     for g in range(GROUPS):
-        middle = jnp.where(
-            lane8 < 64, take(f_in[2, at(g), :], gathered), take(f_in[3, at(g), :], gathered)
-        )
-        around[at(g), :] = jnp.where(edge, f_in[1, at(g), :], middle)
+        around[at(g), :] = jnp.where(edge, f_in[1, at(g), :], take(f_in[2, at(g), :], gathered))
     own = f_in.at[0]
-    shift_groups(0, first_shifts, own, around, groups)
+    for g in groups:
+        first_shifts[4, at(g), :] = own[at(g), :]
+        for d in range(9):
+            if d != 4:
+                lanes = jnp.bitwise_and(tables[d], CELLS - 1)
+                first_shifts[d, at(g), :] = jnp.where(
+                    tables[d] >= CELLS, take(around[at(g), :], lanes), own_shifts[d, at(g), :]
+                )
     observe(0, (own, around), (0, 9))
+
+    for u in range(FIELDS):
+        total = zero
+        for g in groups:
+            total = total + atm[u, at(g), :]
+        mean = allsum(total) / MEM
+        field_mean[u] = mean
+        for g in groups:
+            result[u, at(g), :] = atm[u, at(g), :] - mean
+
+
+    def reduce_covariance(pair):
+        for u in (2 * pair, 2 * pair + 1):
+            for d in range(9):
+                covariance[u, d] = allsum(covariance[u, d])
 
     def first_covariance(pair):
         fields = (2 * pair, 2 * pair + 1)
-        total = [zero, zero]
-        for g in groups:
-            for n, u in enumerate(fields):
-                total[n] = total[n] + atm[u, at(g), :]
-        mean = [allsum(x) / MEM for x in total]
+        if pair > 0:
+            reduce_covariance(pair - 1)
         sums = [[zero] * 9, [zero] * 9]
         for g in groups:
             for n, u in enumerate(fields):
-                block = atm[u, at(g), :] - mean[n]
-                result[u, at(g), :] = block
+                block = result[u, at(g), :]
                 for d in range(9):
                     sums[n][d] = sums[n][d] + first_shifts[d, at(g), :] * block
         for n, u in enumerate(fields):
-            field_mean[u] = mean[n]
             for d in range(9):
-                covariance[u, d] = allsum(sums[n][d])
+                covariance[u, d] = sums[n][d]
         shift_groups(9, other_shifts, own, around, groups[2 * pair : 2 * pair + 2])
 
     for pair in range(pairs):
-        pl.when(always)(functools.partial(first_covariance, pair))
+        region(pair)(functools.partial(first_covariance, pair))
+    reduce_covariance(pairs - 1)
     state[0, MEM:, :] = sst_step(0, own, own[MEM:, :], first_shifts, state.at[0])
     mean = shift(9, 4, own[MEM:, :], around[MEM:, :])
     state[1, MEM:, :] = sst_step(9, other_shifts.at[4], mean, other_shifts, state.at[1])
@@ -700,7 +761,7 @@
         )
 
     for pair in range(pairs):
-        pl.when(always)(functools.partial(first_update, pair))
+        region(pairs + pair)(functools.partial(first_update, pair))
     mean = sst_step(18, state.at[0], state[0, MEM:, :], second_shifts, result.at[FIELDS])
     means[FIELDS] = mean[:1]
     sst_copy = pltpu.make_async_copy(result.at[FIELDS], anom_out.at[FIELDS], mean_sem.at[1])
@@ -725,7 +786,7 @@
         field_copy(pair).start()
 
     for pair in range(pairs):
-        pl.when(always)(functools.partial(second_batch, pair))
+        region(2 * pairs + pair)(functools.partial(second_batch, pair))
     mean_copy = pltpu.make_async_copy(means, mean_out, mean_sem.at[0])
     mean_copy.start()
     sst_copy.wait()
@@ -750,14 +811,15 @@
     vmem = pl.BlockSpec(memory_space=pltpu.VMEM)
     hbm = pl.BlockSpec(memory_space=pltpu.HBM)
     dma = pltpu.SemaphoreType.DMA
-    state, tables = pl.pallas_call(
+    state, own_shifts, tables = pl.pallas_call(
         exchange_kernel,
         out_shape=(
-            jax.ShapeDtypeStruct((4, ROWS, CELLS), f32),
+            jax.ShapeDtypeStruct((3, ROWS, CELLS), f32),
+            jax.ShapeDtypeStruct((9, MEM, CELLS), f32),
             jax.ShapeDtypeStruct((NB, 2, 4, OB, CELLS), f32),
         ),
         in_specs=[hbm] * 9,
-        out_specs=(vmem, vmem),
+        out_specs=(vmem, vmem, vmem),
         scratch_shapes=[
             pltpu.SMEM((1, K), jnp.int32),
             pltpu.VMEM((8, CELLS), jnp.int32),
@@ -775,6 +837,8 @@
             dma((CHUNKS + 8,)),
             dma((24,)),
             dma((9, CHUNKS)),
+            dma((2,)),
+            dma((2,)),
             dma((4,)),
             dma((9,)),
             dma((9,)),
@@ -805,7 +869,7 @@
             jax.ShapeDtypeStruct((COMP, 1, CELLS), f32),
             jax.ShapeDtypeStruct((COMP, MEM, CELLS), f32),
         ),
-        in_specs=[vmem] * 4,
+        in_specs=[vmem] * 5,
         out_specs=(hbm, hbm),
         scratch_shapes=[
             pltpu.VMEM((ROWS, CELLS), f32),
@@ -822,7 +886,7 @@
             dma((2,)),
         ],
         compiler_params=pltpu.CompilerParams(vmem_limit_bytes=16 * 1024 * 1024),
-    )(state, tables, jnp.asarray(shifts), jnp.transpose(atm_members[0, 0], (1, 0, 2)))
+    )(state, own_shifts, tables, jnp.asarray(shifts), jnp.transpose(atm_members[0, 0], (1, 0, 2)))
     return (mean.reshape(1, 1, COMP, CELLS), jnp.transpose(anomaly, (1, 0, 2))[None, None])
 
 

time: 23.4 us -> 23 us (0.983)
  the two profiles are of different devices: /device:TPU:7 before, /device:TPU:37 now
where the time goes in v5:
time: 23 us; the launch traced here: 22.9 us
  Pallas kernels  22.2 us (97%)
  between operations  0.67 us (3%)
    pallas_call x1, Pallas kernels, local(): pl.pallas_call(exchange_kernel, out_shape=(jax.ShapeDtypeStruct((3, ROWS,...  18.4 us
    pallas_call x1, Pallas kernels, local(): pl.pallas_call(update_kernel, out_shape=(jax.ShapeDtypeStruct((COMP, 1, C...  3.76 us

profile of v5, /device:TPU:37, one launch (start us, length us, event | category | flops | bytes accessed | tf_op | source)
XLA Modules:
  0.0 22.9 jit_solution(14843745334373815268)
XLA Ops:
  0.6 0.0 copy-start
  0.6 0.0 copy-start.1
  0.7 18.4 %shard_map.122 = (f32[3,88,128]{2,1,0:T(8,128)S(1)}, f32[9,80,128]{2,1,0:T(8,128)S(1)}, f32[2,2,4,32,128]{4,3,2,1,0:T(8,128)S(1)}) custom-call(s32[1,4]{1,0:T(1,128)} %bitcast.20, bf16[80,1024]{1,0:T(8,128)(2,1)} %bitcast.19, bf16[4,1024,128]{2,1,0:T(8,128)(2,1)} %bitcast.18, s32[1,64]{1,0:T(1,128)} %bitcast.21, f32[1,64]{1,0:T(1,128)} %bitcast.22, ...), custom_call_target="tpu_custom_call" | custom-call | tf_op jit(solution)/shard_map/pallas_call | solution.py:814
  19.1 0.0 copy-done
  19.1 0.0 copy-done.1
  19.1 3.8 %shard_map.123 = (f32[13,1,128]{2,1,0:T(1,128)}, f32[13,80,128]{2,1,0:T(8,128)}) custom-call(f32[3,88,128]{2,1,0:T(8,128)S(1)} %get-tuple-element.7.f_in, f32[9,80,128]{2,1,0:T(8,128)S(1)} %get-tuple-element.8.own_shifts, f32[2,2,4,32,128]{4,3,2,1,0:T(8,128)S(1)} %get-tuple-element.9.obs, s32[28,8,128]{2,1,0:T(8,128)S(1)} %copy-done.1, ...), custom_call_target="tpu_custom_call" | custom-call | tf_op jit(solution)/shard_map/pallas_call | solution.py:866
Async XLA Ops:
  0.6 18.5 %copy-start = (f32[1,1,80,12,128]{4,2,3,1,0:T(8,128)S(1)}, f32[1,1,80,12,128]{4,2,3,1,0:T(8,128)}, u32[]{:S(2)}) copy-start(f32[1,1,80,12,128]{4,2,3,1,0:T(8,128)} %param.11) | copy-start | bytes 1474564
  0.6 18.5 %copy-start.1 = (s32[28,8,128]{2,1,0:T(8,128)S(1)}, s32[28,8,128]{2,1,0:T(8,128)}, u32[]{:S(2)}) copy-start(s32[28,8,128]{2,1,0:T(8,128)} %constant.5.clone.tables) | copy-start | bytes 344068

commit v6 on v5

--- a/solution.py
+++ b/solution.py
@@ -316,12 +316,13 @@
         for c in range(piece[0], piece[0] + piece[1]):
             acc[...] += product(dx, dy, c)
 
-    def from_y(piece, with_away):
+    def from_y(piece, with_away, between=lambda: None):
         def one(dy, is_far):
             arrived(piece, 0, dy)
             send(is_far, False, piece, 0, dy, mate, 0)
 
         one(near, False)
+        between()
         when_far(lambda: one(far, True))
         if with_away:
 
@@ -330,16 +331,14 @@
                 when_far(lambda: both_copy(piece, away, piece[0]).start())
                 when_no_far(lambda: send(None, True, piece, 0, near, away, 0))
 
-    from_y(FIRST, True)
-    meta_copy(0, near, 0).start()
-    when_far(lambda: meta_copy(0, far, 1).start())
-
-    @when_away
-    def _():
+    def from_away():
         arrived(THIRD, away, 0)
         send(False, True, THIRD, away, 0, 0, near)
         when_far(lambda: send(True, True, THIRD, away, 0, 0, far))
 
+    from_y(FIRST, True, lambda: when_away(from_away))
+    meta_copy(0, near, 0).start()
+    when_far(lambda: meta_copy(0, far, 1).start())
     from_y(SECOND, True)
     arrived(WHOLE, mate, 0)
     add(mate, 0, WHOLE)
@@ -402,6 +401,40 @@
             east = jnp.where(pair == (s + 7) % 8, moved, east)
         pack_y[0, 8 * block : 8 * block + 8, :] = west
         pack_y[1, 8 * block : 8 * block + 8, :] = east
+    def halo_y(dx, dy):
+        side = (dy + 1) // 2
+        return pltpu.make_async_remote_copy(
+            src_ref=pack_y.at[side],
+            dst_ref=in_y.at[side, 1 - dx],
+            send_sem=halo_send.at[slot(dx, dy)],
+            recv_sem=halo_recv.at[slot(-dx, -dy)],
+            device_id=device(dx, dy),
+            device_id_type=MESH,
+        )
+
+    def halo_x(dx):
+        side = (dx + 1) // 2
+        return pltpu.make_async_remote_copy(
+            src_ref=pack_x.at[side],
+            dst_ref=in_x.at[side],
+            send_sem=halo_send.at[slot(dx, 0)],
+            recv_sem=halo_recv.at[slot(-dx, 0)],
+            device_id=device(dx, 0),
+            device_id_type=MESH,
+        )
+
+    @when_away
+    def _():
+        when_far(lambda: halo_y(away, far).start())
+        halo_y(away, near).start()
+
+    @when_far
+    def _():
+        halo_y(mate, far).start()
+        halo_y(0, far).start()
+
+    halo_y(mate, near).start()
+    halo_y(0, near).start()
     for block in range(3):
         north = jnp.zeros((8, CELLS), jnp.float32)
         south = north
@@ -413,40 +446,6 @@
         pack_x[0, 8 * block : 8 * block + 8, :] = north
         pack_x[1, 8 * block : 8 * block + 8, :] = south
 
-    def halo_y(dx, dy):
-        side = (dy + 1) // 2
-        return pltpu.make_async_remote_copy(
-            src_ref=pack_y.at[side],
-            dst_ref=in_y.at[side, 1 - dx],
-            send_sem=halo_send.at[slot(dx, dy)],
-            recv_sem=halo_recv.at[slot(-dx, -dy)],
-            device_id=device(dx, dy),
-            device_id_type=MESH,
-        )
-
-    def halo_x(dx):
-        side = (dx + 1) // 2
-        return pltpu.make_async_remote_copy(
-            src_ref=pack_x.at[side],
-            dst_ref=in_x.at[side],
-            send_sem=halo_send.at[slot(dx, 0)],
-            recv_sem=halo_recv.at[slot(-dx, 0)],
-            device_id=device(dx, 0),
-            device_id_type=MESH,
-        )
-
-    @when_away
-    def _():
-        when_far(lambda: halo_y(away, far).start())
-        halo_y(away, near).start()
-
-    @when_far
-    def _():
-        halo_y(mate, far).start()
-        halo_y(0, far).start()
-
-    halo_y(mate, near).start()
-    halo_y(0, near).start()
     when_away(lambda: halo_x(away).start())
     halo_x(mate).start()
 

time: 23 us -> 22.9 us (level)
  the two profiles are of different devices: /device:TPU:37 before, /device:TPU:7 now
where the time goes in v6:
time: 22.9 us; the launch traced here: 22.7 us
  Pallas kernels  22 us (96%)
  between operations  0.67 us (3%)
    pallas_call x1, Pallas kernels, local(): pl.pallas_call(exchange_kernel, out_shape=(jax.ShapeDtypeStruct((3, ROWS,...  18.3 us
    pallas_call x1, Pallas kernels, local(): pl.pallas_call(update_kernel, out_shape=(jax.ShapeDtypeStruct((COMP, 1, C...  3.76 us

profile of v6, /device:TPU:7, one launch (start us, length us, event | category | flops | bytes accessed | tf_op | source)
XLA Modules:
  0.0 22.7 jit_solution(18319860277071859573)
XLA Ops:
  0.6 0.0 copy-start
  0.6 0.0 copy-start.1
  0.7 18.3 %shard_map.122 = (f32[3,88,128]{2,1,0:T(8,128)S(1)}, f32[9,80,128]{2,1,0:T(8,128)S(1)}, f32[2,2,4,32,128]{4,3,2,1,0:T(8,128)S(1)}) custom-call(s32[1,4]{1,0:T(1,128)} %bitcast.20, bf16[80,1024]{1,0:T(8,128)(2,1)} %bitcast.19, bf16[4,1024,128]{2,1,0:T(8,128)(2,1)} %bitcast.18, s32[1,64]{1,0:T(1,128)} %bitcast.21, f32[1,64]{1,0:T(1,128)} %bitcast.22, ...), custom_call_target="tpu_custom_call" | custom-call | tf_op jit(solution)/shard_map/pallas_call | solution.py:813
  18.9 0.0 copy-done
  18.9 0.0 copy-done.1
  18.9 3.8 %shard_map.123 = (f32[13,1,128]{2,1,0:T(1,128)}, f32[13,80,128]{2,1,0:T(8,128)}) custom-call(f32[3,88,128]{2,1,0:T(8,128)S(1)} %get-tuple-element.7.f_in, f32[9,80,128]{2,1,0:T(8,128)S(1)} %get-tuple-element.8.own_shifts, f32[2,2,4,32,128]{4,3,2,1,0:T(8,128)S(1)} %get-tuple-element.9.obs, s32[28,8,128]{2,1,0:T(8,128)S(1)} %copy-done.1, ...), custom_call_target="tpu_custom_call" | custom-call | tf_op jit(solution)/shard_map/pallas_call | solution.py:865
Async XLA Ops:
  0.6 18.3 %copy-start = (f32[1,1,80,12,128]{4,2,3,1,0:T(8,128)S(1)}, f32[1,1,80,12,128]{4,2,3,1,0:T(8,128)}, u32[]{:S(2)}) copy-start(f32[1,1,80,12,128]{4,2,3,1,0:T(8,128)} %param.11) | copy-start | bytes 1474564
  0.6 18.3 %copy-start.1 = (s32[28,8,128]{2,1,0:T(8,128)S(1)}, s32[28,8,128]{2,1,0:T(8,128)}, u32[]{:S(2)}) copy-start(s32[28,8,128]{2,1,0:T(8,128)} %constant.5.clone.tables) | copy-start | bytes 344068
